TPU v7x, 32 devices: a whole 2x2x4 slice. The times are simulated.
32 devices in a mesh: dp: 8 (over z, y), mp: 4 (over x, core).
Axes of the slice: x: 2, y: 2, z: 4, core: 2. Of those that a mesh axis runs over, the one named last changes fastest.
Arguments:
- tokens: bfloat16 [8192, 768], P('dp'), may hold values from -6 to 6
- segments: int32 [16, 512], P('dp'), may hold values from 0 to 7, never falling along the last dimension, each value on 1 to 128 neighbouring positions
- logits_in: bfloat16 [16, 12, 512, 512], P('dp', 'mp'), may hold values from -6 to 6
- w_qkv: bfloat16 [768, 3, 768], P('dp', None, 'mp'), may hold values from -0.21875 to 0.21875
- w_out: bfloat16 [768, 768], P('mp', 'dp'), may hold values from -1.75 to 1.75
- w_up: bfloat16 [768, 3072], P('dp', 'mp'), may hold values from -0.21875 to 0.21875
- w_down: bfloat16 [3072, 768], P('mp', 'dp'), may hold values from -0.15625 to 0.15625
- head_bias: bfloat16 [2, 768], P(None, ('mp', 'dp')), may hold values from -3 to 3
- ff_bias: bfloat16 [3072], P(('mp', 'dp')), may hold values from -3 to 3
- norm_gains: bfloat16 [2, 768], P(None, 'dp'), may hold values from 0.25 to 1.75
- shift_biases: bfloat16 [4, 768], P(None, 'dp'), may hold values from -3 to 3
- grad_out: bfloat16 [8192, 768], P('dp'), may hold values from -6 to 6
- grad_logits: bfloat16 [16, 12, 512, 512], P('dp', 'mp'), may hold values from -0.1796875 to 0.1796875
Outputs:
- mixed: bfloat16 [8192, 768], P('dp')
- logits_out: bfloat16 [16, 12, 512, 512], P('dp', 'mp')
- grad_tokens: bfloat16 [8192, 768], P('dp')
- grad_logits_in: bfloat16 [16, 12, 512, 512], P('dp', 'mp')
- g_w_qkv: float32 [768, 3, 768], P('dp', None, 'mp')
- g_w_out: float32 [768, 768], P('mp', 'dp')
- g_w_up: float32 [768, 3072], P('dp', 'mp')
- g_w_down: float32 [3072, 768], P('mp', 'dp')
- g_head_bias: float32 [2, 768], P(None, ('mp', 'dp'))
- g_ff_bias: float32 [3072], P(('mp', 'dp'))
- g_norm_gains: float32 [2, 768], P(None, 'dp')
- g_shift_biases: float32 [4, 768], P(None, 'dp')
Inputs may be any that keep to these rules, and one draw needn't show every extreme that they name: `segments`: within a packed row the ids never fall; each id covers at most 128 consecutive positions and some id of each row covers exactly that many; tokens attend only to tokens of their own id.
All inputs are finite; a program needn't handle non-finite values.
Results may differ from a plain program's by a relative error of at most 0.018.
Values may be sent and summed in bfloat16 or wider, within the bound.
A program may use at most 192 MiB of HBM per device.

v0:
```python
import jax
import jax.numpy as jnp
from jax import lax
from jax.sharding import PartitionSpec as P

MB = 2


epsilon = 1e-05
masked_value = -10000.0


def norm_rows(hidden, gain, shift):
    center = hidden - jnp.mean(hidden, axis=-1, keepdims=True)
    spread = jnp.mean(center * center, axis=-1, keepdims=True)
    return center * lax.rsqrt(spread + epsilon) * gain + shift


def gelu_exact(value):
    return 0.5 * value * (1.0 + lax.erf(value * 0.7071067811865476))


def add_trees(first_tree, second_tree):
    if first_tree is None:
        return second_tree
    return jax.tree.map(jnp.add, first_tree, second_tree)


def micro_step(whole, block_tokens, block_segments, block_logits, block_grad, block_grad_logits):
    qkv_weight, out_weight, up_weight, down_weight, bias_heads, bias_hidden, gains, shifts = whole
    seq_count = block_segments.shape[0]
    length = block_segments.shape[1]
    feature = block_tokens.shape[1]
    row_count = block_tokens.shape[0]
    local_heads = block_logits.shape[1]
    flat_qkv = qkv_weight.reshape(feature, -1)
    local_cols = flat_qkv.shape[1] // 3
    head_size = local_cols // local_heads
    gain_rows = gains.astype(jnp.float32)
    shift_rows = shifts.astype(jnp.float32)
    head_rows = bias_heads.astype(jnp.float32)
    shape_heads = (seq_count, length, local_heads, head_size)
    token_float = block_tokens.astype(jnp.float32)
    projected = jnp.dot(block_tokens, flat_qkv, preferred_element_type=jnp.float32)
    query = (projected[:, :local_cols] + head_rows[0]).astype(jnp.bfloat16).reshape(shape_heads)
    keys = projected[:, local_cols : 2 * local_cols].astype(jnp.bfloat16).reshape(shape_heads)
    values = (
        (projected[:, 2 * local_cols :] + head_rows[1]).astype(jnp.bfloat16).reshape(shape_heads)
    )
    same = block_segments[:, :, None] == block_segments[:, None, :]
    mask = jnp.where(same, 0.0, masked_value).astype(jnp.float32)[:, None]
    incoming = block_logits.astype(jnp.float32)
    raw = (
        jnp.einsum("sqhd,skhd->shqk", query, keys, preferred_element_type=jnp.float32) * 0.125
        + incoming
    )
    shifted = raw + mask
    top = jnp.max(shifted, axis=-1, keepdims=True)
    expo = jnp.exp(shifted - top)
    total = jnp.sum(expo, axis=-1, keepdims=True)
    log_total = top + jnp.log(total)
    context = jnp.einsum(
        "shqk,skhd->sqhd",
        (expo / total).astype(jnp.bfloat16),
        values,
        preferred_element_type=jnp.float32,
    )
    context = context.reshape(row_count, local_cols).astype(jnp.bfloat16)
    attn_total = lax.psum(jnp.dot(context, out_weight, preferred_element_type=jnp.float32), "mp")
    first_pre = attn_total + shift_rows[0] + token_float
    normed = norm_rows(first_pre, gain_rows[0], shift_rows[1]).astype(jnp.bfloat16)
    hidden_pre = jnp.dot(
        normed, up_weight, preferred_element_type=jnp.float32
    ) + bias_hidden.astype(jnp.float32)
    activated = gelu_exact(hidden_pre).astype(jnp.bfloat16)
    ffn_total = lax.psum(jnp.dot(activated, down_weight, preferred_element_type=jnp.float32), "mp")
    second_pre = ffn_total + shift_rows[2] + normed.astype(jnp.float32)
    cotangent = block_grad.astype(jnp.float32)
    mixed_part = norm_rows(second_pre, gain_rows[1], shift_rows[3]).astype(jnp.bfloat16)
    unused_second, second_pull = jax.vjp(norm_rows, second_pre, gain_rows[1], shift_rows[3])
    grad_second, grad_gain_two, grad_shift_two = second_pull(cotangent)
    branch_part = grad_second.astype(jnp.bfloat16)
    grad_bias_two = jnp.sum(branch_part.astype(jnp.float32), axis=0)
    grad_down = jnp.einsum("rf,rd->fd", activated, branch_part, preferred_element_type=jnp.float32)
    grad_act = jnp.einsum("rd,fd->rf", branch_part, down_weight, preferred_element_type=jnp.float32)
    unused_gelu, gelu_pull = jax.vjp(gelu_exact, hidden_pre)
    grad_hidden = gelu_pull(grad_act)[0].astype(jnp.bfloat16)
    grad_bias_hidden = jnp.sum(grad_hidden.astype(jnp.float32), axis=0)
    grad_up = jnp.einsum("rd,rf->df", normed, grad_hidden, preferred_element_type=jnp.float32)
    hidden_terms = jnp.einsum(
        "rf,df->rd", grad_hidden, up_weight, preferred_element_type=jnp.float32
    )
    grad_normed = grad_second + lax.psum(hidden_terms, "mp")
    unused_first, first_pull = jax.vjp(norm_rows, first_pre, gain_rows[0], shift_rows[1])
    grad_first, grad_gain_one, grad_shift_one = first_pull(grad_normed)
    grad_attn = grad_first.astype(jnp.bfloat16)
    grad_bias_out = jnp.sum(grad_attn.astype(jnp.float32), axis=0)
    grad_out_weight = jnp.einsum(
        "rc,rd->cd", context, grad_attn, preferred_element_type=jnp.float32
    )
    grad_context = jnp.einsum(
        "rd,cd->rc", grad_attn, out_weight, preferred_element_type=jnp.float32
    )
    grad_context = grad_context.astype(jnp.bfloat16).reshape(shape_heads)
    raw_again = (
        jnp.einsum("sqhd,skhd->shqk", query, keys, preferred_element_type=jnp.float32) * 0.125
        + incoming
    )
    prob = jnp.exp(raw_again + mask - log_total)
    grad_prob = jnp.einsum(
        "sqhd,skhd->shqk", grad_context, values, preferred_element_type=jnp.float32
    )
    grad_raw = prob * (
        grad_prob - jnp.sum(prob * grad_prob, axis=-1, keepdims=True)
    ) + block_grad_logits.astype(jnp.float32)
    grad_raw_low = grad_raw.astype(jnp.bfloat16)
    grad_query = (
        jnp.einsum("shqk,skhd->sqhd", grad_raw_low, keys, preferred_element_type=jnp.float32)
        * 0.125
    )
    grad_keys = (
        jnp.einsum("shqk,sqhd->skhd", grad_raw_low, query, preferred_element_type=jnp.float32)
        * 0.125
    )
    grad_values = jnp.einsum(
        "shqk,sqhd->skhd",
        prob.astype(jnp.bfloat16),
        grad_context,
        preferred_element_type=jnp.float32,
    )
    grad_query = grad_query.astype(jnp.bfloat16).reshape(row_count, local_cols)
    grad_keys = grad_keys.astype(jnp.bfloat16).reshape(row_count, local_cols)
    grad_values = grad_values.astype(jnp.bfloat16).reshape(row_count, local_cols)
    grad_proj = jnp.concatenate([grad_query, grad_keys, grad_values], axis=1)
    grad_qkv = jnp.einsum(
        "rd,rc->dc", block_tokens, grad_proj, preferred_element_type=jnp.float32
    ).reshape(qkv_weight.shape)
    grad_heads = jnp.stack(
        [
            jnp.sum(grad_query.astype(jnp.float32), axis=0),
            jnp.sum(grad_values.astype(jnp.float32), axis=0),
        ]
    )
    input_terms = jnp.einsum("rc,dc->rd", grad_proj, flat_qkv, preferred_element_type=jnp.float32)
    grad_inputs = grad_first + lax.psum(input_terms.astype(jnp.bfloat16), "mp").astype(jnp.float32)
    results = (mixed_part, raw.astype(jnp.bfloat16), grad_inputs.astype(jnp.bfloat16), grad_raw_low)
    grads = (
        grad_qkv,
        grad_out_weight,
        grad_up,
        grad_down,
        grad_heads,
        grad_bias_hidden,
        jnp.stack([grad_gain_one, grad_gain_two]),
        jnp.stack([grad_bias_out, grad_shift_one, grad_bias_two, grad_shift_two]),
    )
    return (results, grads)


def shards(
    tokens,
    segments,
    logits_in,
    w_qkv,
    w_out,
    w_up,
    w_down,
    head_bias,
    ff_bias,
    norm_gains,
    shift_biases,
    grad_out,
    grad_logits,
):
    seq_count = segments.shape[0] // MB
    row_count = seq_count * segments.shape[1]
    collected = []
    totals = None
    for micro in range(MB):
        whole = (
            lax.all_gather(w_qkv, "dp", axis=0, tiled=True),
            lax.all_gather(w_out, "dp", axis=1, tiled=True),
            lax.all_gather(w_up, "dp", axis=0, tiled=True),
            lax.all_gather(w_down, "dp", axis=1, tiled=True),
            lax.all_gather(head_bias, "dp", axis=1, tiled=True),
            lax.all_gather(ff_bias, "dp", axis=0, tiled=True),
            lax.all_gather(norm_gains, "dp", axis=1, tiled=True),
            lax.all_gather(shift_biases, "dp", axis=1, tiled=True),
        )
        first_row = micro * row_count
        first_seq = micro * seq_count
        results, grads = micro_step(
            whole,
            tokens[first_row : first_row + row_count],
            segments[first_seq : first_seq + seq_count],
            logits_in[first_seq : first_seq + seq_count],
            grad_out[first_row : first_row + row_count],
            grad_logits[first_seq : first_seq + seq_count],
        )
        totals = add_trees(totals, grads)
        collected.append(results)
    totals = (
        lax.psum_scatter(totals[0], "dp", scatter_dimension=0, tiled=True),
        lax.psum_scatter(totals[1], "dp", scatter_dimension=1, tiled=True),
        lax.psum_scatter(totals[2], "dp", scatter_dimension=0, tiled=True),
        lax.psum_scatter(totals[3], "dp", scatter_dimension=1, tiled=True),
        lax.psum_scatter(totals[4], "dp", scatter_dimension=1, tiled=True),
        lax.psum_scatter(totals[5], "dp", scatter_dimension=0, tiled=True),
        lax.psum_scatter(totals[6], "dp", scatter_dimension=1, tiled=True),
        lax.psum_scatter(totals[7], "dp", scatter_dimension=1, tiled=True),
    )
    mixed = jnp.concatenate([item[0] for item in collected], axis=0)
    logits_out = jnp.concatenate([item[1] for item in collected], axis=0)
    grad_tokens = jnp.concatenate([item[2] for item in collected], axis=0)
    grad_logits_in = jnp.concatenate([item[3] for item in collected], axis=0)
    return (
        mixed,
        logits_out,
        grad_tokens,
        grad_logits_in,
        totals[0],
        totals[1],
        totals[2],
        totals[3],
        totals[4],
        totals[5],
        totals[6],
        totals[7],
    )


def solution(mesh):
    return jax.shard_map(
        shards,
        mesh=mesh,
        in_specs=(
            P("dp", None),
            P("dp", None),
            P("dp", "mp", None, None),
            P("dp", None, "mp"),
            P("mp", "dp"),
            P("dp", "mp"),
            P("mp", "dp"),
            P(None, ("mp", "dp")),
            P(("mp", "dp")),
            P(None, "dp"),
            P(None, "dp"),
            P("dp", None),
            P("dp", "mp", None, None),
        ),
        out_specs=(
            P("dp", None),
            P("dp", "mp", None, None),
            P("dp", None),
            P("dp", "mp", None, None),
            P("dp", None, "mp"),
            P("mp", "dp"),
            P("dp", "mp"),
            P("mp", "dp"),
            P(None, ("mp", "dp")),
            P(("mp", "dp")),
            P(None, "dp"),
            P(None, "dp"),
        ),
        check_vma=False,
    )
```

profile of v0, /device:TPU:0, one launch (start us, length us, event | category | flops | bytes accessed | tf_op | source)
XLA Modules:
  0.0 818.1 jit_solution(586682431443566388)
XLA Ops:
  9.1 40.5 %all_gather.32 = bf16[768,3,192]{2,1,0:T(4,128)(2,1)} all-gather(bf16[96,3,192]{2,1,0:T(4,128)(2,1)S(1)} %copy.80), channel_id=1, replica_groups=mesh['dp'=8,'mp'=4] {'dp'}, dimensions={0}, use_global_device_ids=true | all-gather | bytes 995328 | tf_op jit(solution)/shard_map/all_gather | solution.py:181
  49.6 2.7 copy.81
  55.6 19.0 %all-gather = bf16[8,24,2]{1,2,0:T(2,128)(2,1)S(1)} all-gather(bf16[1,24,2]{1,2,0:T(2,128)(2,1)S(1)} %bitcast.273), channel_id=1, replica_groups=mesh['dp'=8,'mp'=4] {'dp'}, dimensions={0}, use_global_device_ids=true | all-gather | bytes 864 | tf_op jit(solution)/shard_map/all_gather | solution.py:185
  74.9 31.1 %all_gather.34 = bf16[192,768]{0,1:T(8,128)(2,1)S(1)} all-gather(bf16[192,96]{0,1:T(8,128)(2,1)S(1)} %copy.85), channel_id=1, replica_groups=mesh['dp'=8,'mp'=4] {'dp'}, dimensions={1}, use_global_device_ids=true | all-gather | bytes 331776 | tf_op jit(solution)/shard_map/all_gather | solution.py:182
  116.5 2.4 add_reduce_fusion
  130.9 17.2 %all-reduce = bf16[768]{0:T(1024)(128)(2,1)S(1)} all-reduce(bf16[768]{0:T(1024)(128)(2,1)S(1)} %dynamic-update-slice), channel_id=1, replica_groups=mesh['dp'=8,'mp'=4] {'dp'}, use_global_device_ids=true, to_apply=%add | all-reduce | flops 768 | bytes 3072
  148.7 18.9 %all-gather.2 = bf16[8,96,2]{1,2,0:T(2,128)(2,1)S(1)} all-gather(bf16[1,96,2]{1,2,0:T(2,128)(2,1)} %bitcast.274), channel_id=1, replica_groups=mesh['dp'=8,'mp'=4] {'dp'}, dimensions={0}, use_global_device_ids=true | all-gather | bytes 3456 | tf_op jit(solution)/shard_map/all_gather | solution.py:187
  169.7 16.8 %all-gather.1 = bf16[8,96,4]{1,2,0:T(4,128)(2,1)S(1)} all-gather(bf16[1,96,4]{1,2,0:T(4,128)(2,1)} %bitcast.272), channel_id=1, replica_groups=mesh['dp'=8,'mp'=4] {'dp'}, dimensions={0}, use_global_device_ids=true | all-gather | bytes 6912 | tf_op jit(solution)/shard_map/all_gather | solution.py:188
  190.0 3.5 all-reduce.17.cloned.1.call-done
  193.5 3.0 fusion.101
  200.3 3.9 multiply_convert_fusion.1
  206.4 4.0 all-gather.8.cloned.1.call-done
  210.4 3.6 fusion.109
  216.1 66.9 %all-reduce.15.cloned.1.call-done = (f32[512,768]{1,0:T(8,128)}, f32[512,768]{1,0:T(8,128)}) async-done(((f32[512,768]{1,0:T(8,128)}, f32[512,768]{1,0:T(8,128)}), (f32[512,768]{1,0:T(8,128)}, f32[512,768]{1,0:T(8,128)})) %all-reduce.15.cloned.1.call-update) | async-done | bytes 3145744 | tf_op jit(solution)/shard_map/psum | solution.py:76
  283.0 2.8 fusion.99
  289.3 2.5 fusion.98
  304.2 3.9 fusion.103
  308.1 2.6 copy.119
  310.7 2.6 copy.120
  322.4 50.3 %all-reduce.13.cloned.1.call-done = (f32[512,768]{1,0:T(8,128)}, f32[512,768]{1,0:T(8,128)}) async-done(((f32[512,768]{1,0:T(8,128)}, f32[512,768]{1,0:T(8,128)}), (f32[512,768]{1,0:T(8,128)}, f32[512,768]{1,0:T(8,128)})) %all-reduce.13.cloned.1.call-update) | async-done | bytes 3145744 | tf_op jit(solution)/shard_map/psum | solution.py:93
  372.7 4.7 multiply_reduce_fusion.1
  393.9 2.3 fusion.1
  419.8 3.0 copy.98
  424.2 2.8 pad_maximum_fusion.2
  429.2 4.8 copy.99
  436.0 4.8 copy.100
  440.8 21.6 %all-reduce.3 = (f32[2,192]{1,0:T(2,128)S(1)}, f32[768]{0:T(1024)S(1)}) all-reduce(f32[2,192]{1,0:T(2,128)S(1)} %maximum_add_fusion.2, f32[768]{0:T(1024)S(1)} %add.360), channel_id=6, replica_groups=mesh['dp'=8,'mp'=4] {'dp'}, use_global_device_ids=true, to_apply=%region_38.39.clone | all-reduce | flops 1152 | bytes 9216
  465.1 61.1 %reduce-scatter.24.cloned.1.call-done = f32[96,4]{1,0:T(8,128)} async-done(((f32[768,4]{1,0:T(8,128)}), f32[96,4]{1,0:T(8,128)}) %reduce-scatter.24.cloned.1.call-update) | async-done | bytes 1552
  531.0 60.8 %reduce-scatter.20.cloned.1.call-done = f32[96,192]{1,0:T(8,128)} async-done(((f32[768,192]{1,0:T(8,128)}), f32[96,192]{1,0:T(8,128)}) %reduce-scatter.20.cloned.1.call-update) | async-done | bytes 73744
  593.5 71.3 %reduce-scatter.16.cloned.1.call-done = f32[96,768]{1,0:T(8,128)} async-done(((f32[768,768]{1,0:T(8,128)}), f32[96,768]{1,0:T(8,128)}) %reduce-scatter.16.cloned.1.call-update) | async-done | bytes 294928 | tf_op jit(solution)/shard_map/reduce_scatter | solution.py:205
  664.7 72.9 %reduce-scatter.18.cloned.1.call-done = f32[768,96]{0,1:T(8,128)} async-done(((f32[768,768]{0,1:T(8,128)}), f32[768,96]{0,1:T(8,128)}) %reduce-scatter.18.cloned.1.call-update) | async-done | bytes 294928 | tf_op jit(solution)/shard_map/reduce_scatter | solution.py:206
  737.7 72.8 %reduce-scatter.14.cloned.1.call-done = f32[96,3,192]{2,0,1:T(8,128)} async-done(((f32[768,3,192]{2,0,1:T(8,128)}), f32[96,3,192]{2,0,1:T(8,128)}) %reduce-scatter.14.cloned.1.call-update) | async-done | bytes 221200 | tf_op jit(solution)/shard_map/reduce_scatter | solution.py:203
  (392 shorter events, 117.9 us)
Async XLA Ops:
  8.0 185.4 %all-reduce.17.cloned.1.call-start = ((), (), s32[]{:S(2)}) async-start(), calls=%async_computation.16 | async-start | bytes 6291456 | tf_op jit(solution)/shard_map/psum | solution.py:69
  54.0 20.7 %copy-start.113 = (s32[2,512]{1,0:T(2,128)S(1)}, s32[2,512]{1,0:T(2,128)}, u32[]{:S(2)}) copy-start(s32[2,512]{1,0:T(2,128)} %param.14) | copy-start | bytes 12292
  54.0 20.8 %copy-start.79 = (bf16[192,96]{1,0:T(8,128)(2,1)S(1)}, bf16[192,96]{1,0:T(8,128)(2,1)}, u32[]{:S(2)}) copy-start(bf16[192,96]{1,0:T(8,128)(2,1)} %param.17) | copy-start | bytes 110596
  74.8 36.8 %copy-start.38 = (bf16[2,3,512,512]{3,2,1,0:T(8,128)(2,1)S(1)}, bf16[2,3,512,512]{3,2,1,0:T(8,128)(2,1)}, u32[]{:S(2)}) copy-start(bf16[2,3,512,512]{3,2,1,0:T(8,128)(2,1)} %param.15) | copy-start | bytes 9437188
  116.4 5.6 copy-start.48
  116.4 7.0 copy-start.64
  127.6 72.7 %all-gather.6.cloned.1.call-start = ((), (), s32[]{:S(2)}) async-start(), calls=%async_computation.6 | async-start | bytes 1327104 | tf_op jit(solution)/shard_map/all_gather | solution.py:183
  128.2 82.3 %all-gather.8.cloned.1.call-start = ((), (), s32[]{:S(2)}) async-start(), calls=%async_computation.7 | async-start | bytes 1327104 | tf_op jit(solution)/shard_map/all_gather | solution.py:184
  128.7 154.3 %all-reduce.15.cloned.1.call-start = ((), (), s32[]{:S(2)}) async-start(), calls=%async_computation.15 | async-start | bytes 6291456 | tf_op jit(solution)/shard_map/psum | solution.py:76
  169.7 28.2 %copy-start.73 = (f32[768]{0:T(1024)}, f32[768]{0:T(1024)S(1)}, u32[]{:S(2)}) copy-start(f32[768]{0:T(1024)S(1)} %get-tuple-element.83) | copy-start | bytes 9220
  216.0 67.0 %copy-start.98 = (f32[768]{0:T(1024)S(1)}, f32[768]{0:T(1024)}, u32[]{:S(2)}) copy-start(f32[768]{0:T(1024)} %get-tuple-element.79) | copy-start | bytes 9220
  216.1 156.6 %all-reduce.13.cloned.1.call-start = ((), (), s32[]{:S(2)}) async-start(), calls=%async_computation.14 | async-start | bytes 6291456 | tf_op jit(solution)/shard_map/psum | solution.py:93
  292.6 6.6 copy-start.41
  303.9 159.7 %reduce-scatter.22.cloned.1.call-start = ((), (), s32[]{:S(2)}) async-start(), calls=%async_computation.12 | async-start | bytes 442368
  372.7 4.8 copy-start.88
  372.7 4.8 copy-start.3
  372.7 4.8 copy-start.5
  372.7 4.9 copy-start.74
  372.7 4.9 copy-start.76
  372.7 4.9 copy-start.78
  372.7 4.9 copy-start.82
  372.7 4.9 copy-start.84
  379.0 6.2 copy-start.14
  399.0 127.2 %reduce-scatter.24.cloned.1.call-start = ((), (), s32[]{:S(2)}) async-start(), calls=%async_computation.13 | async-start | bytes 442368
  400.2 127.4 %all-reduce.19.cloned.1.call-start = ((), (), s32[]{:S(2)}) async-start(), calls=%async_computation.17 | async-start | bytes 3145728 | tf_op jit(solution)/shard_map/psum | solution.py:145
  403.7 188.1 %reduce-scatter.20.cloned.1.call-start = ((), (), s32[]{:S(2)}) async-start(), calls=%async_computation.11 | async-start | bytes 884736
  406.7 258.0 %reduce-scatter.16.cloned.1.call-start = ((), (), s32[]{:S(2)}) async-start(), calls=%async_computation.9 | async-start | bytes 2654208 | tf_op jit(solution)/shard_map/reduce_scatter | solution.py:205
  411.1 326.5 %reduce-scatter.18.cloned.1.call-start = ((), (), s32[]{:S(2)}) async-start(), calls=%async_computation.10 | async-start | bytes 2654208 | tf_op jit(solution)/shard_map/reduce_scatter | solution.py:206
  415.8 394.6 %reduce-scatter.14.cloned.1.call-start = ((), (), s32[]{:S(2)}) async-start(), calls=%async_computation.8 | async-start | bytes 2654208 | tf_op jit(solution)/shard_map/reduce_scatter | solution.py:203
  429.2 4.8 copy-start.13
  436.0 91.7 %copy-start.17 = (f32[512,768]{1,0:T(8,128)S(1)}, f32[512,768]{1,0:T(8,128)}, u32[]{:S(2)}) copy-start(f32[512,768]{1,0:T(8,128)} %copy-done.16) | copy-start | bytes 4718596
  436.0 91.7 %copy-start.94 = (f32[512]{0:T(512)S(1)}, f32[512]{0:T(512)}, u32[]{:S(2)}) copy-start(f32[512]{0:T(512)} %copy-done.93) | copy-start | bytes 6148
  (102 other events, 210.8 us)
Sparse Core Ops, SparseCore 0:
  127.7 65.7 all-reduce.16
  216.2 66.8 all-reduce.14
  304.1 68.5 all-reduce.12
  403.8 42.9 all-reduce.18
Sparse Core Ops, SparseCore 1:
  130.2 38.5 all-gather.5
  170.8 39.5 all-gather.7
  399.1 62.4 reduce-scatter.21
  464.8 61.3 reduce-scatter.23
  529.5 62.3 reduce-scatter.19
  595.9 68.8 reduce-scatter.15
  668.7 68.9 reduce-scatter.17
  741.6 68.8 reduce-scatter.13
where the time goes:
time: 826 us; the launch traced here: 818 us
  waiting for transfers between devices  465 us (56%)
  blocking collectives  165 us (20%)
  local copies, waits for them, and re-layouts  68.3 us (8%)
  matrix products  55.6 us (7%)
  other arithmetic  44.2 us (5%)
  between operations  19 us (2%)
    unnamed x15, waiting for transfers between devices  123 us
    reduce_scatter x1, waiting for transfers between devices, shards(): lax.psum_scatter(totals[3], 'dp', scatter_dimension=1, tiled=True)  72.9 us
    reduce_scatter x1, waiting for transfers between devices, shards(): lax.psum_scatter(totals[0], 'dp', scatter_dimension=0, tiled=True)  72.8 us
    reduce_scatter x1, waiting for transfers between devices, shards(): lax.psum_scatter(totals[2], 'dp', scatter_dimension=0, tiled=True)  71.3 us
    psum x1, waiting for transfers between devices, micro_step(): lax.psum(jnp.dot(activated, down_weight, preferred_element_type=jnp.float...  66.9 us
    psum x1, waiting for transfers between devices, micro_step(): grad_normed = grad_second + lax.psum(hidden_terms, 'mp')  50.3 us
    unnamed x263, local copies, waits for them, and re-layouts  42.1 us
    all_gather x1, blocking collectives, shards(): lax.all_gather(w_qkv, 'dp', axis=0, tiled=True)  40.5 us
  transfers between devices with their start and end apart: 12, of which 9 were waited for; matrix products, arithmetic and copies ran while one was open for 10% of the time, Pallas kernels for 0%

commit v1 on v0

--- a/solution.py
+++ b/solution.py
@@ -1,10 +1,16 @@
+import functools
+
 import jax
 import jax.numpy as jnp
 from jax import lax
+from jax.experimental import pallas as pl
+from jax.experimental.pallas import tpu as pltpu
 from jax.sharding import PartitionSpec as P
 
 MB = 2
-
+MESH = pl.DeviceIdType.MESH
+F32 = jnp.float32
+BF16 = jnp.bfloat16
 
 epsilon = 1e-05
 masked_value = -10000.0
@@ -229,9 +235,666 @@
     )
 
 
+Z, Y, CORES = 4, 2, 2
+TILE = 32
+EDGE = 128
+CHUNK = 256
+COPIES = 96
+
+
+def dot_nn(a, b):
+    return lax.dot_general(a, b, (((1,), (0,)), ((), ())), preferred_element_type=F32)
+
+
+def dot_nt(a, b):
+    return lax.dot_general(a, b, (((1,), (1,)), ((), ())), preferred_element_type=F32)
+
+
+def dot_tn(a, b):
+    return lax.dot_general(a, b, (((0,), (0,)), ((), ())), preferred_element_type=F32)
+
+
+def fold_rows(value):
+    rows, cols = value.shape
+    return jnp.sum(value.reshape(rows // 8, 8, cols), axis=0)
+
+
+class Wires:
+    def __init__(self, send_sem, recv_sem):
+        self.send_sem, self.recv_sem, self.sent, self.drained = send_sem, recv_sem, [], []
+
+    def send(self, src, dst, device):
+        index = len(self.sent)
+        copy = pltpu.make_async_remote_copy(
+            src_ref=src,
+            dst_ref=dst,
+            send_sem=self.send_sem.at[index],
+            recv_sem=self.recv_sem.at[index],
+            device_id=device,
+            device_id_type=MESH,
+        )
+        copy.start()
+        self.sent.append(copy)
+        return copy
+
+    def drain(self, copy):
+        copy.wait_send()
+        self.drained.append(copy)
+
+    def drain_all(self):
+        for copy in self.sent:
+            if not any(copy is done for done in self.drained):
+                copy.wait_send()
+
+
+def layer_kernel(names, dims, *refs):
+    r_ = dict(zip(names, refs, strict=True))
+    L, HEADS, HD, D, FF, C, SH = dims
+    seqs = 2
+    half = L // 2
+    tok, seg, GOUT = r_["tok"], r_["seg"], r_["GOUT"]
+    WA, WU, WD, WO, SMV = r_["WA"], r_["WU"], r_["WD"], r_["WO"], r_["SMV"]
+    Q, K, V, LIN, GLB, PROB = r_["Q"], r_["K"], r_["V"], r_["LIN"], r_["GLB"], r_["PROB"]
+    BIAS, CTXF, CTXR = r_["BIAS"], r_["CTXF"], r_["CTXR"]
+    NORMED, ACT, DG, BR, GH, GAT = r_["NORMED"], r_["ACT"], r_["DG"], r_["BR"], r_["GH"], r_["GAT"]
+    GC, MIX, GT, XH1, R1, GS = r_["GC"], r_["MIX"], r_["GT"], r_["XH1"], r_["R1"], r_["GS"]
+    HB, CS, CR, XS, XR = r_["HB"], r_["CS"], r_["CR"], r_["XS"], r_["XR"]
+    OWN, GP = r_["OWN"], r_["GP"]
+    GQF, GKF, GVF = r_["GQF"], r_["GKF"], r_["GVF"]
+    SMG, SMS, SMR = r_["SMG"], r_["SMS"], r_["SMR"]
+    local_sem = r_["local_sem"]
+
+    dpi, mpi = lax.axis_index("dp"), lax.axis_index("mp")
+    z, y = lax.div(dpi, Y), lax.rem(dpi, Y)
+    x, core = lax.div(mpi, CORES), lax.rem(mpi, CORES)
+    wires = Wires(r_["send_sem"], r_["recv_sem"])
+
+    def dev(zz, yy, xx, cc):
+        return {"dp": zz * Y + yy, "mp": xx * CORES + cc}
+
+    zto = [lax.rem(z + k, Z) for k in range(Z)]
+    zfrom = [lax.rem(z - k + Z, Z) for k in range(Z)]
+    z_dev = [dev(zto[k], y, x, core) for k in range(Z)]
+    y_dev = dev(z, 1 - y, x, core)
+    c_dev = dev(z, y, x, 1 - core)
+    x_dev = dev(z, y, 1 - x, core)
+    d_dev = dev(z, y, 1 - x, 1 - core)
+
+    def local(src, dst, index):
+        copy = pltpu.make_async_copy(src, dst, local_sem.at[index])
+        copy.start()
+        return copy
+
+    load_lin = [local(r_["lin"].at[s], LIN.at[s], s) for s in range(seqs)]
+    load_gout = [
+        local(r_["gout"].at[pl.ds(pl.multiple_of(s * L + core * half, half), half), :], GOUT.at[s], 4 + s)
+        for s in range(seqs)
+    ]
+    load_gl = [local(r_["gl"].at[s], GLB.at[s], 2 + s) for s in range(seqs)]
+
+    barrier = pltpu.get_barrier_semaphore()
+    friends = z_dev[1:] + [y_dev, c_dev, x_dev, d_dev]
+    for friend in friends:
+        pl.semaphore_signal(barrier, inc=1, device_id=friend, device_id_type=MESH)
+    pl.semaphore_wait(barrier, len(friends))
+
+    def rows_of(index):
+        return pl.ds(pl.multiple_of(index * SH, SH), SH)
+
+    class Gather:
+        def __init__(self, src, dst, place):
+            self.src, self.dst, self.place = src, dst, place
+            self.here = place(z * Y + y)
+            self.zs = [wires.send(src, dst.at[self.here], z_dev[k]) for k in range(1, Z)]
+            self.ys = [wires.send(src, dst.at[self.here], y_dev)]
+
+        def keep(self):
+            self.dst[self.here] = self.src[...]
+
+        def forward(self):
+            for k in range(1, Z):
+                self.zs[k - 1].wait_recv()
+                at = self.place(zfrom[k] * Y + y)
+                self.ys.append(wires.send(self.dst.at[at], self.dst.at[at], y_dev))
+
+        def finish(self):
+            for copy in self.ys:
+                copy.wait_recv()
+
+    def by_rows(index):
+        return (rows_of(index), slice(None))
+
+    gather_a = Gather(r_["wa"], WA, lambda i: (slice(None), rows_of(i), slice(None)))
+    gather_s = Gather(r_["sm"], r_["SM"], lambda i: (i,))
+    gather_u = Gather(r_["wu"], WU, by_rows)
+    gather_d = Gather(r_["wd"], WD, by_rows)
+    for gather in (gather_a, gather_s, gather_u, gather_d):
+        gather.keep()
+    gather_a.forward()
+    gather_s.forward()
+    gather_a.finish()
+    gather_s.finish()
+
+    wo_core = wires.send(WA.at[3], WO.at[0], c_dev)
+    wo_x = wires.send(WA.at[3], WO.at[1], x_dev)
+
+    summed = r_["SM"][0].astype(F32)
+    for i in range(1, Z * Y):
+        summed = summed + r_["SM"][i].astype(F32)
+    SMV[...] = summed
+    SMG[...] = jnp.zeros_like(SMG)
+
+    def vec(row, width=D):
+        return SMV[row : row + 1, :width]
+
+    def project(i, carry):
+        rows = pl.ds(pl.multiple_of(i * CHUNK, CHUNK), CHUNK)
+        block = tok[rows, :]
+        Q[rows, :] = (dot_nn(block, WA[0]) + vec(8, C)).astype(BF16)
+        K[rows, :] = dot_nn(block, WA[1]).astype(BF16)
+        V[rows, :] = (dot_nn(block, WA[2]) + vec(9, C)).astype(BF16)
+        return carry
+
+    lax.fori_loop(0, seqs * L // CHUNK, project, 0)
+
+    lanes = lax.broadcasted_iota(jnp.int32, (1, C), 1) // HD
+
+    def head_mask(h):
+        return jnp.where(lanes == h, 1.0, 0.0).astype(BF16)
+
+    blocks = L // EDGE
+    windows = [(max(b - 1, 0) * EDGE, min(b + 2, blocks) * EDGE) for b in range(blocks)]
+
+    def half_of(s, which):
+        return pl.ds(pl.multiple_of(s * L + which * half, half), half)
+
+    def mine(s):
+        return half_of(s, core)
+
+    def theirs(s):
+        return half_of(s, 1 - core)
+
+    def attend(s):
+        base = s * L
+        ids = seg[s : s + 1, :].astype(F32)
+        tall = jnp.transpose(jnp.broadcast_to(ids, (EDGE, L)))
+        for b, (lo, hi) in enumerate(windows):
+            for j in range((hi - lo) // EDGE):
+                near = ids[:, lo + j * EDGE : lo + (j + 1) * EDGE]
+                same = tall[b * EDGE : (b + 1) * EDGE, :] == near
+                BIAS[b * EDGE : (b + 1) * EDGE, j * EDGE : (j + 1) * EDGE] = jnp.where(
+                    same, 0.0, masked_value
+                ).astype(F32)
+        GQF[...] = jnp.zeros_like(GQF)
+        load_lin[s].wait()
+
+        def head(h, carry):
+            pick = head_mask(h)
+            for b, (lo, hi) in enumerate(windows):
+                rows = slice(b * EDGE, (b + 1) * EDGE)
+                query = Q[base + b * EDGE : base + (b + 1) * EDGE, :] * pick
+                score = dot_nt(query, K[base : base + L, :])
+                raw = score * 0.125 + LIN[s, h, rows, :].astype(F32)
+                LIN[s, h, rows, :] = raw.astype(BF16)
+                near = raw[:, lo:hi] + BIAS[rows, : hi - lo]
+                top = jnp.max(near, axis=-1, keepdims=True)
+                expo = jnp.exp(near - top)
+                norm = 1.0 / jnp.sum(expo, axis=-1, keepdims=True)
+                prob = (expo * norm).astype(BF16)
+                PROB[s, h, rows, : hi - lo] = prob
+                GQF[rows, :] += dot_nn(prob, V[base + lo : base + hi, :] * pick)
+            return carry
+
+        lax.fori_loop(0, HEADS, head, 0)
+        CTXF[base : base + L, :] = GQF[...].astype(BF16)
+        store = local(LIN.at[s], r_["logits_out"].at[s], s)
+        parts = [
+            wires.send(CTXF.at[theirs(s), :], CTXR.at[0, s], c_dev),
+            wires.send(CTXF.at[mine(s), :], CTXR.at[1, s], x_dev),
+            wires.send(CTXF.at[theirs(s), :], CTXR.at[2, s], d_dev),
+        ]
+        return store, parts
+
+    def tile_loop(count, body, init):
+        def step(i, carry):
+            return body(pl.multiple_of(i * TILE, TILE), carry)
+
+        return lax.fori_loop(0, count // TILE, step, init)
+
+    def token_rows(s, r):
+        return pl.ds(pl.multiple_of(s * L + core * half + r, TILE), TILE)
+
+    def normalize(value):
+        center = value - jnp.mean(value, axis=-1, keepdims=True)
+        spread = jnp.mean(center * center, axis=-1, keepdims=True)
+        scale = lax.rsqrt(spread + epsilon)
+        return center * scale, scale
+
+    def norm_back(scaled, xhat, scale):
+        flat = jnp.mean(scaled, axis=-1, keepdims=True)
+        tilt = jnp.mean(scaled * xhat, axis=-1, keepdims=True)
+        return scale * (scaled - flat - xhat * tilt)
+
+    def add_small(rows, sums):
+        for row, value in zip(rows, sums, strict=True):
+            SMG[row : row + 1, :] += jnp.sum(value, axis=0, keepdims=True)
+
+    def share(ref, s):
+        return wires.send(ref.at[mine(s), :], ref.at[mine(s), :], c_dev)
+
+    def out_project(s, parts):
+        for copy in parts:
+            copy.wait_recv()
+        HB[...] = dot_nt(CTXF[mine(s), :], WA[3]) + dot_nt(CTXR[0, s], WO[0])
+        HB[...] += dot_nt(CTXR[1, s], WO[1]) + dot_nt(CTXR[2, s], WO[2])
+
+        def body(r, carry):
+            at = pl.ds(r, TILE)
+            first = HB[at, :] + vec(2) + tok[token_rows(s, r), :].astype(F32)
+            xhat, scale = normalize(first)
+            XH1[s, at, :] = xhat
+            R1[s, at, :] = jnp.broadcast_to(scale, (TILE, EDGE))
+            NORMED[token_rows(s, r), :] = (xhat * vec(0) + vec(3)).astype(BF16)
+            return carry
+
+        tile_loop(half, body, 0)
+        return share(NORMED, s)
+
+    def feed_up(s):
+        def block(i, carry):
+            start = s * L + i * CHUNK
+            rows = pl.ds(pl.multiple_of(start, CHUNK), CHUNK)
+            HB[...] = dot_nn(NORMED[rows, :], WU[...]) + vec(10, FF)
+
+            def body(r, inner):
+                to = pl.ds(pl.multiple_of(start + r, TILE), TILE)
+                value = HB[pl.ds(r, TILE), :]
+                cdf = 0.5 * (1.0 + lax.erf(value * 0.7071067811865476))
+                ACT[to, :] = (value * cdf).astype(BF16)
+                DG[to, :] = cdf + value * (jnp.exp(-0.5 * value * value) * 0.3989422804014327)
+                return inner
+
+            return tile_loop(CHUNK, body, carry)
+
+        lax.fori_loop(0, L // CHUNK, block, 0)
+
+    last_sum = [None] * seqs
+
+    class Reduction:
+        def __init__(self, stage, s, product):
+            self.stage, self.s = stage, s
+            before = last_sum[s]
+            if before is not None:
+                wires.drain(before.pair)
+                wires.drain(before.far)
+            last_sum[s] = self
+            CS[s] = product(theirs(s)).astype(BF16)
+            self.pair = wires.send(CS.at[s], CR.at[s], c_dev)
+            OWN[s] = product(mine(s))
+
+        def cross(self):
+            s = self.s
+            self.pair.wait_recv()
+            XS[s] = (OWN[s] + CR[s].astype(F32)).astype(BF16)
+            self.far = wires.send(XS.at[s], XR.at[self.stage, s], x_dev)
+
+        def wait(self):
+            self.far.wait_recv()
+
+        def tile(self, r):
+            at = pl.ds(r, TILE)
+            return XS[self.s, at, :].astype(F32) + XR[self.stage, self.s, at, :].astype(F32)
+
+    def feed_down(s):
+        return Reduction(0, s, lambda rows: dot_nt(ACT[rows, :], WD[...]))
+
+    zeros = jnp.zeros((8, D), F32)
+
+    def norm_two(s, total):
+        total.wait()
+        load_gout[s].wait()
+
+        def body(r, carry):
+            gain, shift, bias = carry
+            rows = token_rows(s, r)
+            second = total.tile(r) + vec(4) + NORMED[rows, :].astype(F32)
+            xhat, scale = normalize(second)
+            MIX[rows, :] = (xhat * vec(1) + vec(5)).astype(BF16)
+            cot = GOUT[s, pl.ds(r, TILE), :].astype(F32)
+            back = norm_back(cot * vec(1), xhat, scale)
+            GS[s, pl.ds(r, TILE), :] = back
+            low = back.astype(BF16)
+            BR[rows, :] = low
+            gain = gain + fold_rows(cot * xhat)
+            shift = shift + fold_rows(cot)
+            bias = bias + fold_rows(low.astype(F32))
+            return gain, shift, bias
+
+        add_small((1, 5, 4), tile_loop(half, body, (zeros, zeros, zeros)))
+        return share(BR, s), share(MIX, s)
+
+    def feed_back(s):
+        def block(i, carry):
+            start = s * L + i * CHUNK
+            rows = pl.ds(pl.multiple_of(start, CHUNK), CHUNK)
+            HB[...] = dot_nn(BR[rows, :], WD[...])
+
+            def body(r, total):
+                to = pl.ds(pl.multiple_of(start + r, TILE), TILE)
+                low = (HB[pl.ds(r, TILE), :] * DG[to, :]).astype(BF16)
+                GH[to, :] = low
+                return total + fold_rows(low.astype(F32))
+
+            return tile_loop(CHUNK, body, carry)
+
+        sums = lax.fori_loop(0, L // CHUNK, block, jnp.zeros((8, FF), F32))
+        SMG[10:11, :FF] += jnp.sum(sums, axis=0, keepdims=True)
+        return Reduction(1, s, lambda rows: dot_nt(GH[rows, :], WU[...]))
+
+    def norm_one_back(s, total):
+        total.wait()
+
+        def body(r, carry):
+            gain, shift, bias = carry
+            at = pl.ds(r, TILE)
+            cot = GS[s, at, :] + total.tile(r)
+            xhat = XH1[s, at, :]
+            back = norm_back(cot * vec(0), xhat, R1[s, at, 0:1])
+            GS[s, at, :] = back
+            low = back.astype(BF16)
+            GAT[token_rows(s, r), :] = low
+            gain = gain + fold_rows(cot * xhat)
+            shift = shift + fold_rows(cot)
+            bias = bias + fold_rows(low.astype(F32))
+            return gain, shift, bias
+
+        add_small((0, 3, 2), tile_loop(half, body, (zeros, zeros, zeros)))
+        return share(GAT, s)
+
+    def attend_back(s):
+        base = s * L
+        all_rows = slice(base, base + L)
+        GC[...] = dot_nn(GAT[all_rows, :], WA[3]).astype(BF16)
+        GQF[...] = jnp.zeros_like(GQF)
+        GKF[...] = jnp.zeros_like(GKF)
+        GVF[...] = jnp.zeros_like(GVF)
+        load_gl[s].wait()
+
+        def head(h, carry):
+            pick = head_mask(h)
+            for b, (lo, hi) in enumerate(windows):
+                rows = slice(b * EDGE, (b + 1) * EDGE)
+                cot = GC[rows, :] * pick
+                grad_prob = dot_nt(cot, V[base + lo : base + hi, :])
+                prob_low = PROB[s, h, rows, : hi - lo]
+                prob = prob_low.astype(F32)
+                term = prob * grad_prob
+                level = jnp.sum(term, axis=-1, keepdims=True)
+                grad = term - prob * level + GLB[s, h, rows, lo:hi].astype(F32)
+                GLB[s, h, rows, lo:hi] = grad.astype(BF16)
+                GVF[lo:hi, :] += dot_tn(prob_low, cot)
+            grad_raw = GLB[s, h]
+            GQF[...] += dot_nn(grad_raw, K[all_rows, :] * pick)
+            GKF[...] += dot_tn(grad_raw, Q[all_rows, :] * pick)
+            return carry
+
+        lax.fori_loop(0, HEADS, head, 0)
+        store = local(GLB.at[s], r_["glin_out"].at[s], 2 + s)
+        for i, ref, scale in ((0, GQF, 0.125), (1, GKF, 0.125), (2, GVF, 1.0)):
+            low = (ref[...] * scale).astype(BF16)
+            GP[i, all_rows, :] = low
+            if i != 1:
+                row = 8 if i == 0 else 9
+                SMG[row : row + 1, :C] += jnp.sum(low.astype(F32), axis=0, keepdims=True)
+
+        def product(rows):
+            total = dot_nt(GP[0, rows, :], WA[0])
+            total = total + dot_nt(GP[1, rows, :], WA[1])
+            return total + dot_nt(GP[2, rows, :], WA[2])
+
+        return store, Reduction(2, s, product)
+
+    def token_grads(s, total):
+        total.wait()
+
+        def body(r, carry):
+            rows = token_rows(s, r)
+            GT[rows, :] = (GS[s, pl.ds(r, TILE), :] + total.tile(r)).astype(BF16)
+            return carry
+
+        tile_loop(half, body, 0)
+        return share(GT, s)
+
+    class Scatter:
+        def __init__(self, tag, fill):
+            self.stage, self.yr = r_["ST" + tag], r_["YR" + tag]
+            self.zs, self.zr = r_["ZS" + tag], r_["ZR" + tag]
+            fill(self.stage)
+            self.send_y = wires.send(self.stage.at[1 - y], self.yr, y_dev)
+
+        def block(self, index):
+            return self.stage[y, index].astype(F32) + self.yr[index].astype(F32)
+
+        def along(self):
+            self.send_y.wait_recv()
+            self.sent = []
+            for k in range(1, Z):
+                self.zs[k - 1] = self.block(zto[k]).astype(BF16)
+                self.sent.append(wires.send(self.zs.at[k - 1], self.zr.at[k - 1], z_dev[k]))
+
+        def finish(self, out):
+            total = self.block(z)
+            for k in range(1, Z):
+                self.sent[k - 1].wait_recv()
+                total = total + self.zr[k - 1].astype(F32)
+            out[...] = total
+
+    def fill_square(left, right):
+        def fill(stage):
+            part = D // 2
+            for i in range(2):
+                product = dot_tn(left[:, i * part : (i + 1) * part], right[...]).astype(BF16)
+                for j in range(part // SH):
+                    index = i * (part // SH) + j
+                    stage[index % Y, index // Y] = product[j * SH : (j + 1) * SH, :]
+
+        return fill
+
+    def fill_heads(stage):
+        for a in range(4):
+            left, right = (GAT, CTXF[...]) if a == 3 else (tok, GP[a])
+            product = dot_tn(left[...], right).astype(BF16)
+            for index in range(Z * Y):
+                stage[index % Y, index // Y, a] = product[index * SH : (index + 1) * SH, :]
+
+    store_l0, parts0 = attend(0)
+    gather_u.forward()
+    store_l1, parts1 = attend(1)
+    gather_d.forward()
+    wo_core.wait_recv()
+    wo_x.wait_recv()
+    wo_d = wires.send(WO.at[1], WO.at[2], c_dev)
+    wo_d.wait_recv()
+    normed0 = out_project(0, parts0)
+    normed1 = out_project(1, parts1)
+    gather_u.finish()
+    normed0.wait_recv()
+    feed_up(0)
+    gather_d.finish()
+    down0 = feed_down(0)
+    normed1.wait_recv()
+    feed_up(1)
+    down0.cross()
+    down1 = feed_down(1)
+    down1.cross()
+    branch0, mix0 = norm_two(0, down0)
+    branch0.wait_recv()
+    back0 = feed_back(0)
+    back0.cross()
+    branch1, mix1 = norm_two(1, down1)
+    branch1.wait_recv()
+    back1 = feed_back(1)
+    back1.cross()
+    scatter_d = Scatter("D", fill_square(BR, ACT))
+    attn0 = norm_one_back(0, back0)
+    attn0.wait_recv()
+    store_g0, token0 = attend_back(0)
+    token0.cross()
+    scatter_d.along()
+    scatter_u = Scatter("U", fill_square(NORMED, GH))
+    attn1 = norm_one_back(1, back1)
+    attn1.wait_recv()
+    store_g1, token1 = attend_back(1)
+    token1.cross()
+    scatter_u.along()
+    scatter_a = Scatter("A", fill_heads)
+    small_core = wires.send(SMG, SMR.at[0], c_dev)
+    mix0.wait_recv()
+    mix1.wait_recv()
+    store_mix = local(MIX, r_["mixed"], 4)
+    share0 = token_grads(0, token0)
+    small_core.wait_recv()
+    upper = lax.broadcasted_iota(jnp.int32, SMG.shape, 0) < 8
+    SMS[0] = SMG[...] + jnp.where(upper, SMR[0], 0.0)
+    small_y = wires.send(SMS.at[0], SMR.at[1], y_dev)
+    scatter_a.along()
+    share1 = token_grads(1, token1)
+    small_y.wait_recv()
+    SMS[1] = SMS[0] + SMR[1]
+    small_z = [wires.send(SMS.at[1], SMR.at[1 + k], z_dev[k]) for k in range(1, Z)]
+    share0.wait_recv()
+    share1.wait_recv()
+    store_gt = local(GT, r_["gtok"], 5)
+    scatter_d.finish(r_["gd"])
+    scatter_u.finish(r_["gu"])
+    scatter_a.finish(r_["ga"])
+    small_total = SMS[1]
+    for k in range(1, Z):
+        small_z[k - 1].wait_recv()
+        small_total = small_total + SMR[1 + k]
+    r_["smg"][...] = small_total
+    for copy in (store_l0, store_l1, store_g0, store_g1, store_mix, store_gt):
+        copy.wait()
+    wires.drain_all()
+
+
+def fused_shards(
+    tokens, segments, logits_in, w_qkv, w_out, w_up, w_down,
+    head_bias, ff_bias, norm_gains, shift_biases, grad_out, grad_logits,
+):
+    rows, D = tokens.shape
+    seqs, L = segments.shape
+    HEADS = logits_in.shape[1]
+    SH, unused, C = w_qkv.shape
+    FF = w_up.shape[1]
+    HD = C // HEADS
+    half = L // 2
+    width = max(D, FF)
+    dpi = lax.axis_index("dp")
+
+    def spread(array):
+        piece = array.shape[1]
+        wide = jnp.tile(array, (1, Z * Y))
+        owner = lax.broadcasted_iota(jnp.int32, wide.shape, 1) // piece
+        wide = jnp.where(owner == dpi, wide, 0)
+        return jnp.pad(wide, ((0, 0), (0, width - wide.shape[1])))
+
+    blank = jnp.zeros((2, width), BF16)
+    small = jnp.concatenate(
+        [
+            spread(norm_gains),
+            spread(shift_biases),
+            blank,
+            spread(head_bias),
+            spread(ff_bias[None]),
+            blank,
+            blank,
+            blank[:1],
+        ],
+        axis=0,
+    )
+    wa = jnp.stack([w_qkv[:, 0], w_qkv[:, 1], w_qkv[:, 2], w_out.T])
+    dma = pltpu.SemaphoreType.DMA
+    vm = pltpu.VMEM
+    inputs = {
+        "tok": tokens, "wa": wa, "wu": w_up, "wd": w_down.T, "sm": small, "seg": segments,
+        "gout": grad_out, "lin": logits_in, "gl": grad_logits,
+    }
+    shape = jax.ShapeDtypeStruct
+    outputs = {
+        "mixed": shape((rows, D), BF16),
+        "logits_out": shape(logits_in.shape, BF16),
+        "gtok": shape((rows, D), BF16),
+        "glin_out": shape(logits_in.shape, BF16),
+        "ga": shape((4, SH, C), F32),
+        "gu": shape((SH, FF), F32),
+        "gd": shape((SH, FF), F32),
+        "smg": shape((16, width), F32),
+    }
+    scratch = {
+        "WA": vm((4, D, C), BF16), "WU": vm((D, FF), BF16), "WD": vm((D, FF), BF16),
+        "SM": vm((Z * Y, 16, width), BF16), "SMV": vm((16, width), F32), "WO": vm((3, D, C), BF16),
+        "GOUT": vm((seqs, half, D), BF16),
+        "Q": vm((rows, C), BF16), "K": vm((rows, C), BF16), "V": vm((rows, C), BF16),
+        "LIN": vm(logits_in.shape, BF16), "GLB": vm(logits_in.shape, BF16),
+        "PROB": vm((seqs, HEADS, L, 3 * EDGE), BF16), "BIAS": vm((L, 3 * EDGE), F32),
+        "CTXF": vm((rows, C), BF16), "CTXR": vm((3, seqs, half, C), BF16),
+        "NORMED": vm((rows, D), BF16), "ACT": vm((rows, FF), BF16), "DG": vm((rows, FF), F32),
+        "BR": vm((rows, D), BF16), "GH": vm((rows, FF), BF16), "GAT": vm((rows, D), BF16),
+        "GC": vm((L, C), BF16), "MIX": vm((rows, D), BF16), "GT": vm((rows, D), BF16),
+        "XH1": vm((seqs, half, D), F32), "R1": vm((seqs, half, EDGE), F32),
+        "GS": vm((seqs, half, D), F32), "HB": vm((CHUNK, width), F32),
+        "OWN": vm((seqs, half, D), F32), "CS": vm((seqs, half, D), BF16),
+        "CR": vm((seqs, half, D), BF16), "XS": vm((seqs, half, D), BF16),
+        "XR": vm((3, seqs, half, D), BF16), "GP": vm((3, rows, C), BF16),
+        "GQF": vm((L, C), F32), "GKF": vm((L, C), F32), "GVF": vm((L, C), F32),
+        "SMG": vm((16, width), F32), "SMS": vm((2, 16, width), F32), "SMR": vm((5, 16, width), F32),
+        "send_sem": dma((COPIES,)), "recv_sem": dma((COPIES,)), "local_sem": dma((8,)),
+    }
+    for tag, block in (("A", (4, SH, C)), ("U", (SH, FF)), ("D", (SH, FF))):
+        scratch["ST" + tag] = vm((Y, Z) + block, BF16)
+        scratch["YR" + tag] = vm((Z,) + block, BF16)
+        scratch["ZS" + tag] = vm((Z - 1,) + block, BF16)
+        scratch["ZR" + tag] = vm((Z - 1,) + block, BF16)
+    near, far = pl.BlockSpec(memory_space=pltpu.VMEM), pl.BlockSpec(memory_space=pl.ANY)
+    distant = ("gout", "lin", "gl", "mixed", "logits_out", "gtok", "glin_out")
+    names = (*inputs, *outputs, *scratch)
+    dims = (L, HEADS, HD, D, FF, C, SH)
+    results = pl.pallas_call(
+        functools.partial(layer_kernel, names, dims),
+        out_shape=tuple(outputs.values()),
+        in_specs=[far if name in distant else near for name in inputs],
+        out_specs=tuple(far if name in distant else near for name in outputs),
+        scratch_shapes=list(scratch.values()),
+        compiler_params=pltpu.CompilerParams(
+            collective_id=0, has_side_effects=True, vmem_limit_bytes=66 * 1000 * 1000
+        ),
+    )(*inputs.values())
+    mixed, logits_out, gtok, glin, ga, gu, gd, smg = results
+
+    def own(first, last, piece):
+        return lax.dynamic_slice(smg, (first, dpi * piece), (last - first, piece))
+
+    return (
+        mixed,
+        logits_out,
+        gtok,
+        glin,
+        jnp.transpose(ga[:3], (1, 0, 2)),
+        ga[3].T,
+        gu,
+        gd.T,
+        own(8, 10, head_bias.shape[1]),
+        own(10, 11, ff_bias.shape[0])[0],
+        own(0, 2, SH),
+        own(2, 6, SH),
+    )
+
+
 def solution(mesh):
+    body = fused_shards if mesh.shape["dp"] == Z * Y and mesh.shape["mp"] == 4 else shards
     return jax.shard_map(
-        shards,
+        body,
         mesh=mesh,
         in_specs=(
             P("dp", None),

time: 826 us -> 196 us (0.24)
  the two profiles are of different devices: /device:TPU:0 before, /device:TPU:24 now
where the time goes in v1:
time: 196 us; the launch traced here: 195 us
  Pallas kernels  169 us (86%)
  local copies, waits for them, and re-layouts  24.3 us (12%)
    pallas_call x1, Pallas kernels, fused_shards(): pl.pallas_call(functools.partial(layer_kernel, names, dims), out_shape=tu...  169 us
    unnamed x18, local copies, waits for them, and re-layouts  11.1 us
    dynamic_slice x3, local copies, waits for them, and re-layouts, own(): return lax.dynamic_slice(smg, (first, dpi * piece), (last - first, piece))  4 us

profile of v1, /device:TPU:24, one launch (start us, length us, event | category | flops | bytes accessed | tf_op | source)
XLA Modules:
  0.0 195.2 jit_solution(122905499180225986)
XLA Ops:
  0.7 0.7 tile.41
  1.3 0.1 tile.42
  1.5 0.7 tile.39
  2.1 0.1 tile.40
  2.2 0.7 tile.16
  2.9 0.1 tile.17
  3.0 0.7 tile.18
  3.7 0.1 tile.38
  3.8 1.3 concatenate.4.refs_4_
  5.1 0.9 copy.25
  6.0 0.9 slice_bitcast_fusion.4
  6.9 0.7 pad_maximum_fusion.refs_1_
  7.6 169.3 %shard_map.220 = (bf16[1024,768]{1,0:T(8,128)(2,1)}, bf16[2,3,512,512]{3,2,1,0:T(8,128)(2,1)}, bf16[1024,768]{1,0:T(8,128)(2,1)}, bf16[2,3,512,512]{3,2,1,0:T(8,...) custom-call(bf16[1024,768]{1,0:T(8,128)(2,1)} %refs_0_.1, ...), custom_call_target="tpu_custom_call" | custom-call | tf_op jit(solution)/shard_map/pallas_call | solution.py:863
  176.9 0.0 copy-start.1
  176.9 1.4 dynamic-slice_bitcast_fusion
  178.4 1.3 constant_dynamic-slice_fusion.1
  179.7 1.3 constant_dynamic-slice_fusion.2
  181.0 1.3 constant_dynamic-slice_fusion
  182.4 0.9 slice_bitcast_fusion.1
  183.3 1.7 slice_bitcast_fusion
  185.0 0.7 copy.26
  185.7 2.7 %copy.33 = bf16[1024,768]{1,0:T(8,128)(2,1)} copy(bf16[1024,768]{1,0:T(8,128)(2,1)} %get-tuple-element.59) | data formatting | bytes 3145728
  188.4 0.0 copy-done.1
  188.4 1.7 copy.34
  190.0 0.9 copy-done.2
  190.9 1.1 copy.35
  192.1 0.0 copy-done
  192.1 1.7 copy.36
  193.7 0.0 copy-done.4
  193.7 0.7 copy.37
  194.5 0.0 copy-done.3
  194.5 0.7 copy.38
  (16 shorter events, 0.1 us)
Async XLA Ops:
  176.9 11.4 %copy-start.1 = (bf16[2,3,512,512]{3,2,1,0:T(8,128)(2,1)S(1)}, bf16[2,3,512,512]{3,2,1,0:T(8,128)(2,1)}, u32[]{:S(2)}) copy-start(bf16[2,3,512,512]{3,2,1,0:T(8,128)(2,1)} %get-tuple-element.60) | copy-start | bytes 9437188
  188.4 2.5 %copy-start.2 = (bf16[1024,768]{1,0:T(8,128)(2,1)S(1)}, bf16[1024,768]{1,0:T(8,128)(2,1)}, u32[]{:S(2)}) copy-start(bf16[1024,768]{1,0:T(8,128)(2,1)} %get-tuple-element.61) | copy-start | bytes 4718596
  188.4 3.7 %copy-start = (bf16[2,3,512,512]{3,2,1,0:T(8,128)(2,1)S(1)}, bf16[2,3,512,512]{3,2,1,0:T(8,128)(2,1)}, u32[]{:S(2)}) copy-start(bf16[2,3,512,512]{3,2,1,0:T(8,128)(2,1)} %get-tuple-element.62) | copy-start | bytes 9437188
  192.1 1.7 copy-start.4
  192.1 2.4 %copy-start.3 = (f32[96,768]{1,0:T(8,128)S(1)}, f32[96,768]{1,0:T(8,128)}, u32[]{:S(2)}) copy-start(f32[96,768]{1,0:T(8,128)} %get-tuple-element.26) | copy-start | bytes 884740

commit v2 on v1

--- a/solution.py
+++ b/solution.py
@@ -239,7 +239,7 @@
 TILE = 32
 EDGE = 128
 CHUNK = 256
-COPIES = 96
+COPIES = 144
 
 
 def dot_nn(a, b):
@@ -262,28 +262,47 @@
 class Wires:
     def __init__(self, send_sem, recv_sem):
         self.send_sem, self.recv_sem, self.sent, self.drained = send_sem, recv_sem, [], []
-
-    def send(self, src, dst, device):
-        index = len(self.sent)
-        copy = pltpu.make_async_remote_copy(
+        self.slots = 0
+
+    def take(self, count):
+        self.slots += count
+        return self.slots - count
+
+    def describe(self, src, dst, device, out, into):
+        return pltpu.make_async_remote_copy(
             src_ref=src,
             dst_ref=dst,
-            send_sem=self.send_sem.at[index],
-            recv_sem=self.recv_sem.at[index],
+            send_sem=self.send_sem.at[out],
+            recv_sem=self.recv_sem.at[into],
             device_id=device,
             device_id_type=MESH,
+        )
+
+    def send(self, src, dst, device, into=None):
+        copy = self.describe(
+            src, dst, device, len(self.sent), self.take(1) if into is None else into
         )
         copy.start()
         self.sent.append(copy)
         return copy
 
+    def send_if(self, condition, src, dst, device, into):
+        copy = self.describe(src, dst, device, len(self.sent), into)
+        pl.when(condition)(copy.start)
+        self.sent.append((copy, condition))
+
+    def arrived(self, ref, device, into):
+        self.describe(ref, ref, device, 0, into).wait_recv()
+
     def drain(self, copy):
         copy.wait_send()
         self.drained.append(copy)
 
     def drain_all(self):
         for copy in self.sent:
-            if not any(copy is done for done in self.drained):
+            if isinstance(copy, tuple):
+                pl.when(copy[1])(copy[0].wait_send)
+            elif not any(copy is done for done in self.drained):
                 copy.wait_send()
 
 
@@ -326,62 +345,154 @@
         return copy
 
     load_lin = [local(r_["lin"].at[s], LIN.at[s], s) for s in range(seqs)]
+    load_tok = local(r_["tok_far"], tok, 6)
     load_gout = [
         local(r_["gout"].at[pl.ds(pl.multiple_of(s * L + core * half, half), half), :], GOUT.at[s], 4 + s)
         for s in range(seqs)
     ]
     load_gl = [local(r_["gl"].at[s], GLB.at[s], 2 + s) for s in range(seqs)]
 
+    def iotas(rows, cols):
+        down = lax.broadcasted_iota(jnp.int32, (rows, cols), 0)
+        return down, lax.broadcasted_iota(jnp.int32, (rows, cols), 1)
+
+    def shifted(rows, cols, by):
+        down, over = iotas(rows, cols)
+        return jnp.where(over - down == by, 1.0, 0.0).astype(BF16)
+
+    PAIR = 2 * EDGE
+    PK, wa = r_["PK"], r_["wa"]
+    even, odd = shifted(C, PAIR, 0), shifted(C, PAIR, PAIR - C)
+    out_low = dot_nt(shifted(SH, SH, 0), r_["wo"][...]).astype(BF16)
+    for at, first, second in ((0, wa[0], wa[2]), (3 * EDGE, wa[1], out_low)):
+        first, second = dot_nn(first, even), dot_nn(second, odd)
+        PK[:, at : at + EDGE] = first[:, :EDGE].astype(BF16)
+        PK[:, at + EDGE : at + PAIR] = (first[:, EDGE:] + second[:, :EDGE]).astype(BF16)
+        PK[:, at + PAIR : at + 3 * EDGE] = second[:, EDGE:].astype(BF16)
+
     barrier = pltpu.get_barrier_semaphore()
     friends = z_dev[1:] + [y_dev, c_dev, x_dev, d_dev]
     for friend in friends:
         pl.semaphore_signal(barrier, inc=1, device_id=friend, device_id_type=MESH)
     pl.semaphore_wait(barrier, len(friends))
 
-    def rows_of(index):
-        return pl.ds(pl.multiple_of(index * SH, SH), SH)
+    near = z - 1 + 2 * lax.div(3 - z, 3)
+    last = 3 * (1 - lax.div(z, 2))
+    order = [near, 6 - z - near - last, last]
 
     class Gather:
         def __init__(self, src, dst, place):
             self.src, self.dst, self.place = src, dst, place
-            self.here = place(z * Y + y)
-            self.zs = [wires.send(src, dst.at[self.here], z_dev[k]) for k in range(1, Z)]
-            self.ys = [wires.send(src, dst.at[self.here], y_dev)]
+            self.z_in, self.y_in = wires.take(Z), wires.take(Z)
+
+        def along(self):
+            here = self.dst.at[self.place(dpi)]
+            for there in order:
+                wires.send(self.src, here, dev(there, y, x, core), self.z_in + z)
+
+        def across(self):
+            wires.send(self.src, self.dst.at[self.place(dpi)], y_dev, self.y_in + z)
 
         def keep(self):
-            self.dst[self.here] = self.src[...]
-
-        def forward(self):
-            for k in range(1, Z):
-                self.zs[k - 1].wait_recv()
-                at = self.place(zfrom[k] * Y + y)
-                self.ys.append(wires.send(self.dst.at[at], self.dst.at[at], y_dev))
+            self.dst[self.place(dpi)] = self.src[...]
+
+        def forward(self, step):
+            origin = order[step]
+            block = self.dst.at[self.place(origin * Y + y)]
+            wires.arrived(block, y_dev, self.z_in + origin)
+            wires.send(block, block, y_dev, self.y_in + origin)
 
         def finish(self):
-            for copy in self.ys:
-                copy.wait_recv()
+            for origin in range(Z):
+                block = self.dst.at[self.place(origin * Y + 1 - y)]
+                wires.arrived(block, y_dev, self.y_in + origin)
+
+    class Line(Gather):
+        def push(self, src, origin, held):
+            block = self.dst.at[self.place(origin * Y + y)]
+            if src is None:
+                src = block
+            ways = ((z < Z - 1, jnp.minimum(z + 1, Z - 1), 0), (z > 0, jnp.maximum(z - 1, 0), 1))
+            for room, there, side in ways:
+                if held is None or held[1] == side:
+                    going = room if held is None else jnp.logical_and(room, held[0])
+                    wires.send_if(going, src, block, dev(there, y, x, core), self.z_in + origin)
+            if held is None:
+                wires.send(src, block, y_dev, self.y_in + origin)
+            else:
+                wires.send_if(held[0], src, block, y_dev, self.y_in + origin)
+
+        def start(self):
+            self.push(self.src, z, None)
+
+        def step(self, hop):
+            for side, origin, held in ((0, z - hop, z >= hop), (1, z + hop, z + hop < Z)):
+                block = self.dst.at[self.place(jnp.clip(origin, 0, Z - 1) * Y + y)]
+
+                @pl.when(held)
+                def arrive():
+                    wires.arrived(block, y_dev, self.z_in + origin)
+
+                self.push(None, jnp.clip(origin, 0, Z - 1), (held, side))
+
+    def rows_of(index):
+        return pl.ds(pl.multiple_of(index * SH, SH), SH)
 
     def by_rows(index):
         return (rows_of(index), slice(None))
 
-    gather_a = Gather(r_["wa"], WA, lambda i: (slice(None), rows_of(i), slice(None)))
-    gather_s = Gather(r_["sm"], r_["SM"], lambda i: (i,))
+    def by_lanes(index):
+        return (slice(None), pl.ds(pl.multiple_of(index * EDGE, EDGE), EDGE))
+
+    SMB, SM = r_["SMB"], r_["SM"]
+    gather_a = Line(PK, WA, by_rows)
+    gather_s = Gather(SMB, SM, by_lanes)
     gather_u = Gather(r_["wu"], WU, by_rows)
     gather_d = Gather(r_["wd"], WD, by_rows)
+
+    gather_a.start()
+
+    blend = r_["BLEND"]
+    blend[...] = jnp.zeros_like(blend)
+    blend[0:2, :SH] = r_["gains"][...].astype(F32)
+    blend[2:6, :SH] = r_["shifts"][...].astype(F32)
+    piece = r_["hbias"].shape[1]
+    blend[8:10, :piece] = r_["hbias"][...].astype(F32)
+    blend[10:11, :SH] = r_["fbias"][...].astype(F32)
+    SMB[...] = blend[...].astype(BF16)
+    gather_s.along()
+    gather_s.across()
+
     for gather in (gather_a, gather_s, gather_u, gather_d):
         gather.keep()
-    gather_a.forward()
-    gather_s.forward()
+    load_tok.wait()
+    gather_a.step(1)
+    for i in range(Z * Y):
+        rows = slice(i * EDGE, (i + 1) * EDGE)
+        down, over = iotas(EDGE, GH.shape[1])
+        GH[rows, :] = jnp.where((over - down == i * SH) & (down < SH), 1.0, 0.0).astype(BF16)
+        down, over = iotas(EDGE, 2 * PAIR)
+        gap = i * piece + jnp.where(over < PAIR, 0, PAIR + PAIR - C)
+        ACT[rows, : 2 * PAIR] = jnp.where(
+            (over - down == gap) & (down < piece), 1.0, 0.0
+        ).astype(BF16)
+
+    gather_a.step(2)
+    gather_a.step(3)
+    for step in range(Z - 1):
+        gather_s.forward(step)
     gather_a.finish()
     gather_s.finish()
-
-    wo_core = wires.send(WA.at[3], WO.at[0], c_dev)
-    wo_x = wires.send(WA.at[3], WO.at[1], x_dev)
-
-    summed = r_["SM"][0].astype(F32)
-    for i in range(1, Z * Y):
-        summed = summed + r_["SM"][i].astype(F32)
-    SMV[...] = summed
+    gather_u.along()
+    gather_d.along()
+    gather_u.across()
+    gather_d.across()
+    outer = WA.at[:, 4 * EDGE : 6 * EDGE]
+    wo_core = wires.send(outer, WO.at[0], c_dev)
+    wo_x = wires.send(outer, WO.at[1], x_dev)
+
+    SMV[...] = dot_nn(SM[...], GH[...])
+    r_["HBV"][...] = dot_nn(SM[...], ACT[:, : 2 * PAIR])
     SMG[...] = jnp.zeros_like(SMG)
 
     def vec(row, width=D):
@@ -390,17 +501,19 @@
     def project(i, carry):
         rows = pl.ds(pl.multiple_of(i * CHUNK, CHUNK), CHUNK)
         block = tok[rows, :]
-        Q[rows, :] = (dot_nn(block, WA[0]) + vec(8, C)).astype(BF16)
-        K[rows, :] = dot_nn(block, WA[1]).astype(BF16)
-        V[rows, :] = (dot_nn(block, WA[2]) + vec(9, C)).astype(BF16)
+        HBV = r_["HBV"]
+        Q[rows, :] = (dot_nn(block, WA[:, :PAIR]) + HBV[8:9, :PAIR]).astype(BF16)
+        V[rows, :] = (dot_nn(block, WA[:, EDGE : 3 * EDGE]) + HBV[9:10, PAIR:]).astype(BF16)
+        K[rows, :] = dot_nn(block, WA[:, 3 * EDGE : 5 * EDGE]).astype(BF16)
         return carry
 
     lax.fori_loop(0, seqs * L // CHUNK, project, 0)
 
-    lanes = lax.broadcasted_iota(jnp.int32, (1, C), 1) // HD
-
-    def head_mask(h):
-        return jnp.where(lanes == h, 1.0, 0.0).astype(BF16)
+    lanes = lax.broadcasted_iota(jnp.int32, (1, PAIR), 1)
+
+    def head_mask(h, start=0):
+        inside = (lanes >= start + h * HD) & (lanes < start + (h + 1) * HD)
+        return jnp.where(inside, 1.0, 0.0).astype(BF16)
 
     blocks = L // EDGE
     windows = [(max(b - 1, 0) * EDGE, min(b + 2, blocks) * EDGE) for b in range(blocks)]
@@ -414,7 +527,7 @@
     def theirs(s):
         return half_of(s, 1 - core)
 
-    def attend(s):
+    def attend(s, between):
         base = s * L
         ids = seg[s : s + 1, :].astype(F32)
         tall = jnp.transpose(jnp.broadcast_to(ids, (EDGE, L)))
@@ -428,8 +541,8 @@
         GQF[...] = jnp.zeros_like(GQF)
         load_lin[s].wait()
 
-        def head(h, carry):
-            pick = head_mask(h)
+        for h in range(HEADS):
+            pick, pick_v = head_mask(h), head_mask(h, PAIR - C)
             for b, (lo, hi) in enumerate(windows):
                 rows = slice(b * EDGE, (b + 1) * EDGE)
                 query = Q[base + b * EDGE : base + (b + 1) * EDGE, :] * pick
@@ -442,10 +555,9 @@
                 norm = 1.0 / jnp.sum(expo, axis=-1, keepdims=True)
                 prob = (expo * norm).astype(BF16)
                 PROB[s, h, rows, : hi - lo] = prob
-                GQF[rows, :] += dot_nn(prob, V[base + lo : base + hi, :] * pick)
-            return carry
-
-        lax.fori_loop(0, HEADS, head, 0)
+                GQF[rows, :] += dot_nn(prob, V[base + lo : base + hi, :] * pick_v)
+            for job in between[h]:
+                job()
         CTXF[base : base + L, :] = GQF[...].astype(BF16)
         store = local(LIN.at[s], r_["logits_out"].at[s], s)
         parts = [
@@ -485,12 +597,12 @@
     def out_project(s, parts):
         for copy in parts:
             copy.wait_recv()
-        HB[...] = dot_nt(CTXF[mine(s), :], WA[3]) + dot_nt(CTXR[0, s], WO[0])
-        HB[...] += dot_nt(CTXR[1, s], WO[1]) + dot_nt(CTXR[2, s], WO[2])
+        HB[...] = dot_nt(CTXF[mine(s), :], outer[...]) + dot_nt(CTXR[0, s], WO[0])
+        OWN[s] = dot_nt(CTXR[1, s], WO[1]) + dot_nt(CTXR[2, s], WO[2])
 
         def body(r, carry):
             at = pl.ds(r, TILE)
-            first = HB[at, :] + vec(2) + tok[token_rows(s, r), :].astype(F32)
+            first = (HB[at, :] + OWN[s, at, :]) + vec(2) + tok[token_rows(s, r), :].astype(F32)
             xhat, scale = normalize(first)
             XH1[s, at, :] = xhat
             R1[s, at, :] = jnp.broadcast_to(scale, (TILE, EDGE))
@@ -551,7 +663,6 @@
     zeros = jnp.zeros((8, D), F32)
 
     def norm_two(s, total):
-        total.wait()
         load_gout[s].wait()
 
         def body(r, carry):
@@ -592,8 +703,6 @@
         return Reduction(1, s, lambda rows: dot_nt(GH[rows, :], WU[...]))
 
     def norm_one_back(s, total):
-        total.wait()
-
         def body(r, carry):
             gain, shift, bias = carry
             at = pl.ds(r, TILE)
@@ -611,20 +720,20 @@
         add_small((0, 3, 2), tile_loop(half, body, (zeros, zeros, zeros)))
         return share(GAT, s)
 
-    def attend_back(s):
+    def attend_back(s, between):
         base = s * L
         all_rows = slice(base, base + L)
-        GC[...] = dot_nn(GAT[all_rows, :], WA[3]).astype(BF16)
+        GC[...] = dot_nn(GAT[all_rows, :], outer[...]).astype(BF16)
         GQF[...] = jnp.zeros_like(GQF)
         GKF[...] = jnp.zeros_like(GKF)
         GVF[...] = jnp.zeros_like(GVF)
         load_gl[s].wait()
 
-        def head(h, carry):
-            pick = head_mask(h)
+        for h in range(HEADS):
+            pick, pick_v = head_mask(h), head_mask(h, PAIR - C)
             for b, (lo, hi) in enumerate(windows):
                 rows = slice(b * EDGE, (b + 1) * EDGE)
-                cot = GC[rows, :] * pick
+                cot = GC[rows, :] * pick_v
                 grad_prob = dot_nt(cot, V[base + lo : base + hi, :])
                 prob_low = PROB[s, h, rows, : hi - lo]
                 prob = prob_low.astype(F32)
@@ -636,27 +745,25 @@
             grad_raw = GLB[s, h]
             GQF[...] += dot_nn(grad_raw, K[all_rows, :] * pick)
             GKF[...] += dot_tn(grad_raw, Q[all_rows, :] * pick)
-            return carry
-
-        lax.fori_loop(0, HEADS, head, 0)
+            for job in between[h]:
+                job()
         store = local(GLB.at[s], r_["glin_out"].at[s], 2 + s)
-        for i, ref, scale in ((0, GQF, 0.125), (1, GKF, 0.125), (2, GVF, 1.0)):
-            low = (ref[...] * scale).astype(BF16)
-            GP[i, all_rows, :] = low
-            if i != 1:
-                row = 8 if i == 0 else 9
-                SMG[row : row + 1, :C] += jnp.sum(low.astype(F32), axis=0, keepdims=True)
+        low_q = (GQF[...] * 0.125).astype(BF16)
+        low_k = (GKF[...] * 0.125).astype(BF16)
+        low_v = GVF[...].astype(BF16)
+        GP[all_rows, :EDGE] = low_q[:, :EDGE]
+        GP[all_rows, EDGE:PAIR] = low_q[:, EDGE:] + low_v[:, :EDGE]
+        GP[all_rows, PAIR : 3 * EDGE] = low_v[:, EDGE:]
+        GP[all_rows, 3 * EDGE :] = low_k
+        SMG[8:9, :PAIR] += jnp.sum(low_q.astype(F32), axis=0, keepdims=True)
+        SMG[9:10, :PAIR] += jnp.sum(low_v.astype(F32), axis=0, keepdims=True)
 
         def product(rows):
-            total = dot_nt(GP[0, rows, :], WA[0])
-            total = total + dot_nt(GP[1, rows, :], WA[1])
-            return total + dot_nt(GP[2, rows, :], WA[2])
+            return dot_nt(GP[rows, :], WA[:, : 5 * EDGE])
 
         return store, Reduction(2, s, product)
 
     def token_grads(s, total):
-        total.wait()
-
         def body(r, carry):
             rows = token_rows(s, r)
             GT[rows, :] = (GS[s, pl.ds(r, TILE), :] + total.tile(r)).astype(BF16)
@@ -670,24 +777,31 @@
             self.stage, self.yr = r_["ST" + tag], r_["YR" + tag]
             self.zs, self.zr = r_["ZS" + tag], r_["ZR" + tag]
             fill(self.stage)
-            self.send_y = wires.send(self.stage.at[1 - y], self.yr, y_dev)
+            self.y_in = [
+                wires.send(self.stage.at[1 - y, zto[k]], self.yr.at[zto[k]], y_dev)
+                for k in (1, 2, 3, 0)
+            ]
+            self.sent = []
 
         def block(self, index):
             return self.stage[y, index].astype(F32) + self.yr[index].astype(F32)
 
-        def along(self):
-            self.send_y.wait_recv()
-            self.sent = []
+        def along(self, k):
+            self.y_in[k - 1].wait_recv()
+            self.zs[k - 1] = self.block(zto[k]).astype(BF16)
+            self.sent.append(wires.send(self.zs.at[k - 1], self.zr.at[k - 1], z_dev[k]))
+
+        def along_all(self):
             for k in range(1, Z):
-                self.zs[k - 1] = self.block(zto[k]).astype(BF16)
-                self.sent.append(wires.send(self.zs.at[k - 1], self.zr.at[k - 1], z_dev[k]))
-
-        def finish(self, out):
+                self.along(k)
+
+        def finish(self):
+            self.y_in[Z - 1].wait_recv()
             total = self.block(z)
             for k in range(1, Z):
                 self.sent[k - 1].wait_recv()
                 total = total + self.zr[k - 1].astype(F32)
-            out[...] = total
+            return total
 
     def fill_square(left, right):
         def fill(stage):
@@ -700,82 +814,156 @@
 
         return fill
 
-    def fill_heads(stage):
-        for a in range(4):
-            left, right = (GAT, CTXF[...]) if a == 3 else (tok, GP[a])
-            product = dot_tn(left[...], right).astype(BF16)
-            for index in range(Z * Y):
-                stage[index % Y, index // Y, a] = product[index * SH : (index + 1) * SH, :]
-
-    store_l0, parts0 = attend(0)
-    gather_u.forward()
-    store_l1, parts1 = attend(1)
-    gather_d.forward()
-    wo_core.wait_recv()
+    def fill_blocks(stage, at, product):
+        wide = product.shape[1]
+        for index in range(Z * Y):
+            stage[index % Y, index // Y, :, at : at + wide] = product[index * SH : (index + 1) * SH, :]
+
+    def fill_first(stage):
+        fill_blocks(stage, 0, dot_tn(tok[...], GP[:, : 3 * EDGE]).astype(BF16))
+
+    def fill_second(stage):
+        keys, outs = dot_tn(tok[...], GP[:, 3 * EDGE :]), r_["OG"]
+        fill_blocks(stage, 0, keys[:, :EDGE].astype(BF16))
+        fill_blocks(stage, EDGE, (keys[:, EDGE:] + outs[:, :EDGE]).astype(BF16))
+        fill_blocks(stage, PAIR, outs[:, EDGE:].astype(BF16))
+
+    def pass_on(gather, step):
+        return lambda: gather.forward(step)
+
+    store_l0, parts0 = attend(0, ((), (pass_on(gather_u, 0),), (pass_on(gather_d, 0),)))
     wo_x.wait_recv()
     wo_d = wires.send(WO.at[1], WO.at[2], c_dev)
+    store_l1, parts1 = attend(1, ((pass_on(gather_u, 1),), (pass_on(gather_d, 1),), ()))
+    gather_u.forward(2)
+    wo_core.wait_recv()
     wo_d.wait_recv()
     normed0 = out_project(0, parts0)
+    gather_d.forward(2)
     normed1 = out_project(1, parts1)
     gather_u.finish()
     normed0.wait_recv()
     feed_up(0)
+    normed1.wait_recv()
+    feed_up(1)
     gather_d.finish()
     down0 = feed_down(0)
-    normed1.wait_recv()
-    feed_up(1)
+    down1 = feed_down(1)
     down0.cross()
-    down1 = feed_down(1)
+    down0.wait()
     down1.cross()
     branch0, mix0 = norm_two(0, down0)
     branch0.wait_recv()
     back0 = feed_back(0)
     back0.cross()
+    down1.wait()
     branch1, mix1 = norm_two(1, down1)
     branch1.wait_recv()
+    scatter_d = Scatter("D", fill_square(BR, ACT))
     back1 = feed_back(1)
+    scatter_u = Scatter("U", fill_square(NORMED, GH))
+    scatter_d.along(1)
+    back0.wait()
     back1.cross()
-    scatter_d = Scatter("D", fill_square(BR, ACT))
     attn0 = norm_one_back(0, back0)
+    scatter_d.along(2)
     attn0.wait_recv()
-    store_g0, token0 = attend_back(0)
+    store_g0, token0 = attend_back(0, ((), (), ()))
     token0.cross()
-    scatter_d.along()
-    scatter_u = Scatter("U", fill_square(NORMED, GH))
+    scatter_d.along(3)
+    back1.wait()
     attn1 = norm_one_back(1, back1)
+    scatter_u.along(1)
     attn1.wait_recv()
-    store_g1, token1 = attend_back(1)
-    token1.cross()
-    scatter_u.along()
-    scatter_a = Scatter("A", fill_heads)
+    r_["OG"][...] = dot_tn(GAT[...], CTXF[...])
+
+    def pass_up(step):
+        return lambda: scatter_u.along(step)
+
+    store_g1, token1 = attend_back(1, ((), (pass_up(2),), (pass_up(3),)))
     small_core = wires.send(SMG, SMR.at[0], c_dev)
-    mix0.wait_recv()
-    mix1.wait_recv()
-    store_mix = local(MIX, r_["mixed"], 4)
-    share0 = token_grads(0, token0)
+    scatter_f = Scatter("F", fill_first)
     small_core.wait_recv()
     upper = lax.broadcasted_iota(jnp.int32, SMG.shape, 0) < 8
     SMS[0] = SMG[...] + jnp.where(upper, SMR[0], 0.0)
     small_y = wires.send(SMS.at[0], SMR.at[1], y_dev)
-    scatter_a.along()
-    share1 = token_grads(1, token1)
+    scatter_g = Scatter("G", fill_second)
+    token0.wait()
+    token1.cross()
+    share0 = token_grads(0, token0)
+    mix0.wait_recv()
+    mix1.wait_recv()
+    store_mix = local(MIX, r_["mixed"], 4)
     small_y.wait_recv()
     SMS[1] = SMS[0] + SMR[1]
     small_z = [wires.send(SMS.at[1], SMR.at[1 + k], z_dev[k]) for k in range(1, Z)]
-    share0.wait_recv()
-    share1.wait_recv()
-    store_gt = local(GT, r_["gtok"], 5)
-    scatter_d.finish(r_["gd"])
-    scatter_u.finish(r_["gu"])
-    scatter_a.finish(r_["ga"])
+    scatter_f.along_all()
+    r_["gd"][...] = scatter_d.finish()
+    r_["gu"][...] = scatter_u.finish()
+    token1.wait()
+    share1 = token_grads(1, token1)
+    scatter_g.along_all()
     small_total = SMS[1]
     for k in range(1, Z):
         small_z[k - 1].wait_recv()
         small_total = small_total + SMR[1 + k]
-    r_["smg"][...] = small_total
+    SMV[...] = small_total
+
+    def own(first, count, width, start=0):
+        value = SMV[first : first + count, start : start + width]
+        for i in range(1, Z * Y):
+            here = SMV[first : first + count, start + i * width : start + (i + 1) * width]
+            value = jnp.where(dpi == i, here, value)
+        return value
+
+    r_["ggains"][...] = own(0, 2, SH)
+    r_["gshifts"][...] = own(2, 4, SH)
+    r_["ghbias"][0:1] = own(8, 1, piece)
+    r_["ghbias"][1:2] = own(9, 1, piece, PAIR - C)
+    r_["gfbias"][...] = own(10, 1, SH)
+    share0.wait_recv()
+    share1.wait_recv()
+    store_gt = local(GT, r_["gtok"], 5)
+    first = scatter_f.finish()
+    r_["ga"][0] = first[:, :C]
+    r_["ga"][2] = first[:, C:]
+    second = scatter_g.finish()
+    r_["ga"][1] = second[:, :C]
+    r_["go"][...] = jnp.transpose(second[:, C:])
     for copy in (store_l0, store_l1, store_g0, store_g1, store_mix, store_gt):
         copy.wait()
     wires.drain_all()
+
+
+def pass_kernel(count, *refs):
+    sources, targets = refs[:count], refs[count : 2 * count]
+    held, sem = refs[2 * count : 3 * count], refs[3 * count]
+    loads = [
+        pltpu.make_async_copy(sources[i], held[i], sem.at[i]) for i in range(count)
+    ]
+    stores = [
+        pltpu.make_async_copy(held[i], targets[i], sem.at[count + i]) for i in range(count)
+    ]
+    for copy in loads:
+        copy.start()
+    for load, store in zip(loads, stores, strict=True):
+        load.wait()
+        store.start()
+    for copy in stores:
+        copy.wait()
+
+
+def pass_through(arrays):
+    count = len(arrays)
+    far = pl.BlockSpec(memory_space=pl.ANY)
+    return pl.pallas_call(
+        functools.partial(pass_kernel, count),
+        out_shape=tuple(jax.ShapeDtypeStruct(a.shape, a.dtype) for a in arrays),
+        in_specs=[far] * count,
+        out_specs=(far,) * count,
+        scratch_shapes=[pltpu.VMEM(a.shape, a.dtype) for a in arrays]
+        + [pltpu.SemaphoreType.DMA((2 * count,))],
+    )(*arrays)
 
 
 def fused_shards(
@@ -790,34 +978,12 @@
     HD = C // HEADS
     half = L // 2
     width = max(D, FF)
-    dpi = lax.axis_index("dp")
-
-    def spread(array):
-        piece = array.shape[1]
-        wide = jnp.tile(array, (1, Z * Y))
-        owner = lax.broadcasted_iota(jnp.int32, wide.shape, 1) // piece
-        wide = jnp.where(owner == dpi, wide, 0)
-        return jnp.pad(wide, ((0, 0), (0, width - wide.shape[1])))
-
-    blank = jnp.zeros((2, width), BF16)
-    small = jnp.concatenate(
-        [
-            spread(norm_gains),
-            spread(shift_biases),
-            blank,
-            spread(head_bias),
-            spread(ff_bias[None]),
-            blank,
-            blank,
-            blank[:1],
-        ],
-        axis=0,
-    )
-    wa = jnp.stack([w_qkv[:, 0], w_qkv[:, 1], w_qkv[:, 2], w_out.T])
     dma = pltpu.SemaphoreType.DMA
     vm = pltpu.VMEM
     inputs = {
-        "tok": tokens, "wa": wa, "wu": w_up, "wd": w_down.T, "sm": small, "seg": segments,
+        "tok_far": tokens, "wa": jnp.transpose(w_qkv, (1, 0, 2)), "wo": w_out, "wu": w_up,
+        "wd": w_down.T, "hbias": head_bias, "fbias": ff_bias[None], "gains": norm_gains,
+        "shifts": shift_biases, "seg": segments,
         "gout": grad_out, "lin": logits_in, "gl": grad_logits,
     }
     shape = jax.ShapeDtypeStruct
@@ -826,38 +992,46 @@
         "logits_out": shape(logits_in.shape, BF16),
         "gtok": shape((rows, D), BF16),
         "glin_out": shape(logits_in.shape, BF16),
-        "ga": shape((4, SH, C), F32),
+        "ga": shape((3, SH, C), F32),
+        "go": shape((C, SH), F32),
         "gu": shape((SH, FF), F32),
         "gd": shape((SH, FF), F32),
-        "smg": shape((16, width), F32),
+        "ghbias": shape(head_bias.shape, F32),
+        "gfbias": shape((1,) + ff_bias.shape, F32),
+        "ggains": shape(norm_gains.shape, F32),
+        "gshifts": shape(shift_biases.shape, F32),
     }
     scratch = {
-        "WA": vm((4, D, C), BF16), "WU": vm((D, FF), BF16), "WD": vm((D, FF), BF16),
-        "SM": vm((Z * Y, 16, width), BF16), "SMV": vm((16, width), F32), "WO": vm((3, D, C), BF16),
+        "tok": vm((rows, D), BF16),
+        "WA": vm((D, 6 * EDGE), BF16), "PK": vm((SH, 6 * EDGE), BF16), "WU": vm((D, FF), BF16),
+        "WD": vm((D, FF), BF16), "BLEND": vm((16, EDGE), F32),
+        "SMB": vm((16, EDGE), BF16), "SM": vm((16, Z * Y * EDGE), BF16),
+        "SMV": vm((16, width), F32), "HBV": vm((16, 4 * EDGE), F32), "WO": vm((3, D, 2 * EDGE), BF16),
         "GOUT": vm((seqs, half, D), BF16),
-        "Q": vm((rows, C), BF16), "K": vm((rows, C), BF16), "V": vm((rows, C), BF16),
+        "Q": vm((rows, 2 * EDGE), BF16), "K": vm((rows, 2 * EDGE), BF16), "V": vm((rows, 2 * EDGE), BF16),
         "LIN": vm(logits_in.shape, BF16), "GLB": vm(logits_in.shape, BF16),
         "PROB": vm((seqs, HEADS, L, 3 * EDGE), BF16), "BIAS": vm((L, 3 * EDGE), F32),
-        "CTXF": vm((rows, C), BF16), "CTXR": vm((3, seqs, half, C), BF16),
+        "CTXF": vm((rows, 2 * EDGE), BF16), "CTXR": vm((3, seqs, half, 2 * EDGE), BF16),
         "NORMED": vm((rows, D), BF16), "ACT": vm((rows, FF), BF16), "DG": vm((rows, FF), F32),
         "BR": vm((rows, D), BF16), "GH": vm((rows, FF), BF16), "GAT": vm((rows, D), BF16),
-        "GC": vm((L, C), BF16), "MIX": vm((rows, D), BF16), "GT": vm((rows, D), BF16),
+        "GC": vm((L, 2 * EDGE), BF16), "MIX": vm((rows, D), BF16), "GT": vm((rows, D), BF16),
         "XH1": vm((seqs, half, D), F32), "R1": vm((seqs, half, EDGE), F32),
         "GS": vm((seqs, half, D), F32), "HB": vm((CHUNK, width), F32),
         "OWN": vm((seqs, half, D), F32), "CS": vm((seqs, half, D), BF16),
         "CR": vm((seqs, half, D), BF16), "XS": vm((seqs, half, D), BF16),
-        "XR": vm((3, seqs, half, D), BF16), "GP": vm((3, rows, C), BF16),
-        "GQF": vm((L, C), F32), "GKF": vm((L, C), F32), "GVF": vm((L, C), F32),
+        "XR": vm((3, seqs, half, D), BF16), "GP": vm((rows, 5 * EDGE), BF16), "OG": vm((D, 2 * EDGE), F32),
+        "GQF": vm((L, 2 * EDGE), F32), "GKF": vm((L, 2 * EDGE), F32), "GVF": vm((L, 2 * EDGE), F32),
         "SMG": vm((16, width), F32), "SMS": vm((2, 16, width), F32), "SMR": vm((5, 16, width), F32),
         "send_sem": dma((COPIES,)), "recv_sem": dma((COPIES,)), "local_sem": dma((8,)),
     }
-    for tag, block in (("A", (4, SH, C)), ("U", (SH, FF)), ("D", (SH, FF))):
+    for tag in "UDFG":
+        block = (SH, FF if tag in "UD" else 3 * EDGE)
         scratch["ST" + tag] = vm((Y, Z) + block, BF16)
         scratch["YR" + tag] = vm((Z,) + block, BF16)
         scratch["ZS" + tag] = vm((Z - 1,) + block, BF16)
         scratch["ZR" + tag] = vm((Z - 1,) + block, BF16)
     near, far = pl.BlockSpec(memory_space=pltpu.VMEM), pl.BlockSpec(memory_space=pl.ANY)
-    distant = ("gout", "lin", "gl", "mixed", "logits_out", "gtok", "glin_out")
+    distant = ("tok_far", "gout", "lin", "gl", "mixed", "logits_out", "gtok", "glin_out")
     names = (*inputs, *outputs, *scratch)
     dims = (L, HEADS, HD, D, FF, C, SH)
     results = pl.pallas_call(
@@ -870,29 +1044,27 @@
             collective_id=0, has_side_effects=True, vmem_limit_bytes=66 * 1000 * 1000
         ),
     )(*inputs.values())
-    mixed, logits_out, gtok, glin, ga, gu, gd, smg = results
-
-    def own(first, last, piece):
-        return lax.dynamic_slice(smg, (first, dpi * piece), (last - first, piece))
-
+    mixed, logits_out, gtok, glin, ga, go, gu, gd, ghbias, gfbias, ggains, gshifts = pass_through(
+        results
+    )
     return (
         mixed,
         logits_out,
         gtok,
         glin,
-        jnp.transpose(ga[:3], (1, 0, 2)),
-        ga[3].T,
+        jnp.transpose(ga, (1, 0, 2)),
+        go,
         gu,
         gd.T,
-        own(8, 10, head_bias.shape[1]),
-        own(10, 11, ff_bias.shape[0])[0],
-        own(0, 2, SH),
-        own(2, 6, SH),
+        ghbias,
+        gfbias[0],
+        ggains,
+        gshifts,
     )
 
 
 def solution(mesh):
-    body = fused_shards if mesh.shape["dp"] == Z * Y and mesh.shape["mp"] == 4 else shards
+    body = fused_shards if mesh.shape["dp"] == Z * Y and mesh.shape["mp"] == 2 * CORES else shards
     return jax.shard_map(
         body,
         mesh=mesh,

time: 196 us -> 155 us (0.79)
  the two profiles are of different devices: /device:TPU:24 before, /device:TPU:0 now
where the time goes in v2:
time: 155 us; the launch traced here: 154 us
  Pallas kernels  154 us (99%)
    pallas_call x1, Pallas kernels, fused_shards(): pl.pallas_call(functools.partial(layer_kernel, names, dims), out_shape=tu...  145 us
    pallas_call x1, Pallas kernels, pass_through(): pl.pallas_call(functools.partial(pass_kernel, count), out_shape=tuple((ja...  8.21 us

profile of v2, /device:TPU:0, one launch (start us, length us, event | category | flops | bytes accessed | tf_op | source)
XLA Modules:
  0.0 154.4 jit_solution(6168624040488134429)
XLA Ops:
  0.6 145.4 %shard_map.220 = (bf16[1024,768]{1,0:T(8,128)(2,1)}, bf16[2,3,512,512]{3,2,1,0:T(8,128)(2,1)}, bf16[1024,768]{1,0:T(8,128)(2,1)}, bf16[2,3,512,512]{3,2,1,0:T(8,...) custom-call(bf16[1024,768]{1,0:T(8,128)(2,1)} %refs_0_.1, ...), custom_call_target="tpu_custom_call" | custom-call | tf_op jit(solution)/shard_map/pallas_call | solution.py:1037
  146.0 8.2 %shard_map.221 = (bf16[1024,768]{1,0:T(8,128)(2,1)}, bf16[2,3,512,512]{3,2,1,0:T(8,128)(2,1)}, bf16[1024,768]{1,0:T(8,128)(2,1)}, bf16[2,3,512,512]{3,2,1,0:T(8,...) custom-call(bf16[1024,768]{1,0:T(8,128)(2,1)} %get-tuple-element.36., ...), custom_call_target="tpu_custom_call" | custom-call | tf_op jit(solution)/shard_map/pallas_call | solution.py:959

commit v3 on v2

--- a/solution.py
+++ b/solution.py
@@ -1,4 +1,5 @@
 import functools
+import types
 
 import jax
 import jax.numpy as jnp
@@ -239,7 +240,7 @@
 TILE = 32
 EDGE = 128
 CHUNK = 256
-COPIES = 144
+SENDS, ARRIVALS, LOADS = 144, 116, 16
 
 
 def dot_nn(a, b):
@@ -307,26 +308,26 @@
 
 
 def layer_kernel(names, dims, *refs):
-    r_ = dict(zip(names, refs, strict=True))
+    r_ = types.SimpleNamespace(**dict(zip(names, refs, strict=True)))
     L, HEADS, HD, D, FF, C, SH = dims
     seqs = 2
     half = L // 2
-    tok, seg, GOUT = r_["tok"], r_["seg"], r_["GOUT"]
-    WA, WU, WD, WO, SMV = r_["WA"], r_["WU"], r_["WD"], r_["WO"], r_["SMV"]
-    Q, K, V, LIN, GLB, PROB = r_["Q"], r_["K"], r_["V"], r_["LIN"], r_["GLB"], r_["PROB"]
-    BIAS, CTXF, CTXR = r_["BIAS"], r_["CTXF"], r_["CTXR"]
-    NORMED, ACT, DG, BR, GH, GAT = r_["NORMED"], r_["ACT"], r_["DG"], r_["BR"], r_["GH"], r_["GAT"]
-    GC, MIX, GT, XH1, R1, GS = r_["GC"], r_["MIX"], r_["GT"], r_["XH1"], r_["R1"], r_["GS"]
-    HB, CS, CR, XS, XR = r_["HB"], r_["CS"], r_["CR"], r_["XS"], r_["XR"]
-    OWN, GP = r_["OWN"], r_["GP"]
-    GQF, GKF, GVF = r_["GQF"], r_["GKF"], r_["GVF"]
-    SMG, SMS, SMR = r_["SMG"], r_["SMS"], r_["SMR"]
-    local_sem = r_["local_sem"]
+    tok, seg, GOUT = r_.tok, r_.seg, r_.GOUT
+    WA, WU, WD, WO, SMV = r_.WA, r_.WU, r_.WD, r_.WO, r_.SMV
+    Q, K, V, LIN, GLB, PROB = r_.Q, r_.K, r_.V, r_.logits_out, r_.glin_out, r_.PROB
+    BIAS, CTXF, CTXR = r_.BIAS, r_.CTXF, r_.CTXR
+    NORMED, ACT, DG, BR, GH, GAT = r_.NORMED, r_.ACT, r_.DG, r_.BR, r_.GH, r_.GAT
+    GC, MIX, GT, XH1, R1, GS = r_.GC, r_.mixed, r_.gtok, r_.XH1, r_.R1, r_.GS
+    HB, CS, CR, XS, XR = r_.HB, r_.CS, r_.CR, r_.XS, r_.XR
+    OWN, GP = r_.OWN, r_.GP
+    GQF, GKF, GVF = r_.GQF, r_.GKF, r_.GVF
+    SMG, SMS, SMR = r_.SMG, r_.SMS, r_.SMR
+    local_sem = r_.local_sem
 
     dpi, mpi = lax.axis_index("dp"), lax.axis_index("mp")
     z, y = lax.div(dpi, Y), lax.rem(dpi, Y)
     x, core = lax.div(mpi, CORES), lax.rem(mpi, CORES)
-    wires = Wires(r_["send_sem"], r_["recv_sem"])
+    wires = Wires(r_.send_sem, r_.recv_sem)
 
     def dev(zz, yy, xx, cc):
         return {"dp": zz * Y + yy, "mp": xx * CORES + cc}
@@ -339,41 +340,62 @@
     x_dev = dev(z, y, 1 - x, core)
     d_dev = dev(z, y, 1 - x, 1 - core)
 
-    def local(src, dst, index):
-        copy = pltpu.make_async_copy(src, dst, local_sem.at[index])
-        copy.start()
-        return copy
-
-    load_lin = [local(r_["lin"].at[s], LIN.at[s], s) for s in range(seqs)]
-    load_tok = local(r_["tok_far"], tok, 6)
-    load_gout = [
-        local(r_["gout"].at[pl.ds(pl.multiple_of(s * L + core * half, half), half), :], GOUT.at[s], 4 + s)
-        for s in range(seqs)
-    ]
-    load_gl = [local(r_["gl"].at[s], GLB.at[s], 2 + s) for s in range(seqs)]
-
-    def iotas(rows, cols):
-        down = lax.broadcasted_iota(jnp.int32, (rows, cols), 0)
-        return down, lax.broadcasted_iota(jnp.int32, (rows, cols), 1)
-
-    def shifted(rows, cols, by):
-        down, over = iotas(rows, cols)
-        return jnp.where(over - down == by, 1.0, 0.0).astype(BF16)
-
-    PAIR = 2 * EDGE
-    PK, wa = r_["PK"], r_["wa"]
-    even, odd = shifted(C, PAIR, 0), shifted(C, PAIR, PAIR - C)
-    out_low = dot_nt(shifted(SH, SH, 0), r_["wo"][...]).astype(BF16)
-    for at, first, second in ((0, wa[0], wa[2]), (3 * EDGE, wa[1], out_low)):
-        first, second = dot_nn(first, even), dot_nn(second, odd)
-        PK[:, at : at + EDGE] = first[:, :EDGE].astype(BF16)
-        PK[:, at + EDGE : at + PAIR] = (first[:, EDGE:] + second[:, :EDGE]).astype(BF16)
-        PK[:, at + PAIR : at + 3 * EDGE] = second[:, EDGE:].astype(BF16)
-
     barrier = pltpu.get_barrier_semaphore()
     friends = z_dev[1:] + [y_dev, c_dev, x_dev, d_dev]
     for friend in friends:
         pl.semaphore_signal(barrier, inc=1, device_id=friend, device_id_type=MESH)
+
+    locals_used = []
+
+    def local(src, dst):
+        copy = pltpu.make_async_copy(src, dst, local_sem.at[len(locals_used)])
+        copy.start()
+        locals_used.append(copy)
+        return copy
+
+    def rows_of(index):
+        return pl.ds(pl.multiple_of(index * SH, SH), SH)
+
+    load_first = [local(r_.wa_far, r_.wa), local(r_.wo_far, r_.wo)]
+    load_vecs = [
+        local(r_.hbias_far, r_.hbias),
+        local(r_.fbias_far, r_.fbias),
+        local(r_.gains_far, r_.gains),
+        local(r_.shifts_far, r_.shifts),
+    ]
+    load_up = local(r_.wu, WU.at[rows_of(dpi), :])
+    load_down = local(r_.wd, WD.at[rows_of(dpi), :])
+    load_tok = local(r_.tok_far, tok)
+    load_seg = local(r_.seg_far, seg)
+    load_lin = [local(r_.lin.at[s], LIN.at[s]) for s in range(seqs)]
+    load_gout = [
+        local(
+            r_.gout.at[pl.ds(pl.multiple_of(s * L + core * half, half), half), :],
+            GOUT.at[s],
+        )
+        for s in range(seqs)
+    ]
+    load_gl = [local(r_.gl.at[s], GLB.at[s]) for s in range(seqs)]
+    def iotas(rows, cols):
+        down = lax.broadcasted_iota(jnp.int32, (rows, cols), 0)
+        return down, lax.broadcasted_iota(jnp.int32, (rows, cols), 1)
+
+    def shifted(rows, cols, by):
+        down, over = iotas(rows, cols)
+        return jnp.where(over - down == by, 1.0, 0.0).astype(BF16)
+
+    PAIR = 2 * EDGE
+    wa, here = r_.wa, rows_of(dpi)
+    even, odd = shifted(C, PAIR, 0), shifted(C, PAIR, PAIR - C)
+    for copy in load_first:
+        copy.wait()
+    out_low = dot_nt(shifted(SH, SH, 0), r_.wo[...]).astype(BF16)
+    for at, first, second in ((0, wa[0], wa[2]), (3 * EDGE, wa[1], out_low)):
+        first, second = dot_nn(first, even), dot_nn(second, odd)
+        WA[here, at : at + EDGE] = first[:, :EDGE].astype(BF16)
+        WA[here, at + EDGE : at + PAIR] = (first[:, EDGE:] + second[:, :EDGE]).astype(BF16)
+        WA[here, at + PAIR : at + 3 * EDGE] = second[:, EDGE:].astype(BF16)
+
     pl.semaphore_wait(barrier, len(friends))
 
     near = z - 1 + 2 * lax.div(3 - z, 3)
@@ -381,20 +403,17 @@
     order = [near, 6 - z - near - last, last]
 
     class Gather:
-        def __init__(self, src, dst, place):
-            self.src, self.dst, self.place = src, dst, place
+        def __init__(self, dst, place):
+            self.dst, self.place = dst, place
+            self.own = dst.at[place(dpi)]
             self.z_in, self.y_in = wires.take(Z), wires.take(Z)
 
         def along(self):
-            here = self.dst.at[self.place(dpi)]
             for there in order:
-                wires.send(self.src, here, dev(there, y, x, core), self.z_in + z)
+                wires.send(self.own, self.own, dev(there, y, x, core), self.z_in + z)
 
         def across(self):
-            wires.send(self.src, self.dst.at[self.place(dpi)], y_dev, self.y_in + z)
-
-        def keep(self):
-            self.dst[self.place(dpi)] = self.src[...]
+            wires.send(self.own, self.own, y_dev, self.y_in + z)
 
         def forward(self, step):
             origin = order[step]
@@ -408,65 +427,92 @@
                 wires.arrived(block, y_dev, self.y_in + origin)
 
     class Line(Gather):
-        def push(self, src, origin, held):
-            block = self.dst.at[self.place(origin * Y + y)]
-            if src is None:
-                src = block
-            ways = ((z < Z - 1, jnp.minimum(z + 1, Z - 1), 0), (z > 0, jnp.maximum(z - 1, 0), 1))
-            for room, there, side in ways:
-                if held is None or held[1] == side:
-                    going = room if held is None else jnp.logical_and(room, held[0])
-                    wires.send_if(going, src, block, dev(there, y, x, core), self.z_in + origin)
-            if held is None:
-                wires.send(src, block, y_dev, self.y_in + origin)
-            else:
-                wires.send_if(held[0], src, block, y_dev, self.y_in + origin)
+        turns = True
+
+        def block(self, origin):
+            return self.dst.at[self.place(jnp.clip(origin, 0, Z - 1) * Y + y)]
+
+        def push(self, src, origin, held, side):
+            block = self.block(origin)
+            room, there = ((z < Z - 1, z + 1), (z > 0, z - 1))[side]
+            going = room if held is None else jnp.logical_and(room, held)
+            device = dev(jnp.clip(there, 0, Z - 1), y, x, core)
+            slot = self.z_in + jnp.clip(origin, 0, Z - 1)
+            wires.send_if(going, src, block, device, slot)
 
         def start(self):
-            self.push(self.src, z, None)
+            for side in range(2):
+                self.push(self.own, z, None, side)
 
         def step(self, hop):
             for side, origin, held in ((0, z - hop, z >= hop), (1, z + hop, z + hop < Z)):
-                block = self.dst.at[self.place(jnp.clip(origin, 0, Z - 1) * Y + y)]
+                block = self.block(origin)
+                slot = jnp.clip(origin, 0, Z - 1)
 
                 @pl.when(held)
                 def arrive():
-                    wires.arrived(block, y_dev, self.z_in + origin)
-
-                self.push(None, jnp.clip(origin, 0, Z - 1), (held, side))
+                    wires.arrived(block, y_dev, self.z_in + slot)
+
+                self.push(block, origin, held, side)
+                if self.turns:
+                    wires.send_if(held, block, block, y_dev, self.y_in + slot)
+
+    class PairLine(Line):
+        turns = False
+
+        def __init__(self, dst, place, place_pair):
+            Gather.__init__(self, dst, place)
+            self.place_pair = place_pair
+
+        def block(self, origin):
+            return self.dst.at[self.place_pair(jnp.clip(origin, 0, Z - 1))]
+
+        def meet(self):
+            wires.arrived(self.dst.at[self.place(z * Y + 1 - y)], y_dev, self.y_in + z)
+            self.own = self.block(z)
+            self.start()
 
     def rows_of(index):
         return pl.ds(pl.multiple_of(index * SH, SH), SH)
 
-    def by_rows(index):
-        return (rows_of(index), slice(None))
+    def lanes_of(start, stop):
+        return lambda index: (rows_of(index), slice(start, stop))
 
     def by_lanes(index):
         return (slice(None), pl.ds(pl.multiple_of(index * EDGE, EDGE), EDGE))
 
-    SMB, SM = r_["SMB"], r_["SM"]
-    gather_a = Line(PK, WA, by_rows)
-    gather_s = Gather(SMB, SM, by_lanes)
-    gather_u = Gather(r_["wu"], WU, by_rows)
-    gather_d = Gather(r_["wd"], WD, by_rows)
+    SM = r_.SM
+    gather_a = Line(WA, lanes_of(0, 3 * EDGE))
+    gather_b = Line(WA, lanes_of(3 * EDGE, 6 * EDGE))
+    gather_s = Gather(SM, by_lanes)
+    gather_u = Line(WU, lanes_of(0, FF))
+    cut = FF - PAIR
+    gather_d = Line(WD, lanes_of(0, cut))
+    gather_e = PairLine(
+        WD,
+        lanes_of(cut, FF),
+        lambda i: (pl.ds(pl.multiple_of(i * Y * SH, Y * SH), Y * SH), slice(cut, FF)),
+    )
 
     gather_a.start()
-
-    blend = r_["BLEND"]
+    gather_b.start()
+    gather_a.across()
+    gather_b.across()
+
+    for copy in load_vecs:
+        copy.wait()
+    blend = r_.BLEND
     blend[...] = jnp.zeros_like(blend)
-    blend[0:2, :SH] = r_["gains"][...].astype(F32)
-    blend[2:6, :SH] = r_["shifts"][...].astype(F32)
-    piece = r_["hbias"].shape[1]
-    blend[8:10, :piece] = r_["hbias"][...].astype(F32)
-    blend[10:11, :SH] = r_["fbias"][...].astype(F32)
-    SMB[...] = blend[...].astype(BF16)
+    blend[0:2, :SH] = r_.gains[...].astype(F32)
+    blend[2:6, :SH] = r_.shifts[...].astype(F32)
+    piece = r_.hbias.shape[1]
+    blend[8:10, :piece] = r_.hbias[...].astype(F32)
+    blend[10:11, :SH] = r_.fbias[...].astype(F32)
+    SM[by_lanes(dpi)] = blend[...].astype(BF16)
     gather_s.along()
     gather_s.across()
-
-    for gather in (gather_a, gather_s, gather_u, gather_d):
-        gather.keep()
-    load_tok.wait()
     gather_a.step(1)
+    gather_b.step(1)
     for i in range(Z * Y):
         rows = slice(i * EDGE, (i + 1) * EDGE)
         down, over = iotas(EDGE, GH.shape[1])
@@ -478,21 +524,25 @@
         ).astype(BF16)
 
     gather_a.step(2)
+    gather_b.step(2)
     gather_a.step(3)
+    gather_b.step(3)
+    load_up.wait()
+    load_down.wait()
+    gather_u.start()
     for step in range(Z - 1):
         gather_s.forward(step)
     gather_a.finish()
+    gather_b.finish()
     gather_s.finish()
-    gather_u.along()
-    gather_d.along()
     gather_u.across()
-    gather_d.across()
+    gather_e.across()
     outer = WA.at[:, 4 * EDGE : 6 * EDGE]
     wo_core = wires.send(outer, WO.at[0], c_dev)
     wo_x = wires.send(outer, WO.at[1], x_dev)
 
     SMV[...] = dot_nn(SM[...], GH[...])
-    r_["HBV"][...] = dot_nn(SM[...], ACT[:, : 2 * PAIR])
+    r_.HBV[...] = dot_nn(SM[...], ACT[:, : 2 * PAIR])
     SMG[...] = jnp.zeros_like(SMG)
 
     def vec(row, width=D):
@@ -501,12 +551,16 @@
     def project(i, carry):
         rows = pl.ds(pl.multiple_of(i * CHUNK, CHUNK), CHUNK)
         block = tok[rows, :]
-        HBV = r_["HBV"]
+        HBV = r_.HBV
         Q[rows, :] = (dot_nn(block, WA[:, :PAIR]) + HBV[8:9, :PAIR]).astype(BF16)
         V[rows, :] = (dot_nn(block, WA[:, EDGE : 3 * EDGE]) + HBV[9:10, PAIR:]).astype(BF16)
         K[rows, :] = dot_nn(block, WA[:, 3 * EDGE : 5 * EDGE]).astype(BF16)
         return carry
 
+    gather_u.step(1)
+    gather_d.start()
+    load_tok.wait()
+    load_seg.wait()
     lax.fori_loop(0, seqs * L // CHUNK, project, 0)
 
     lanes = lax.broadcasted_iota(jnp.int32, (1, PAIR), 1)
@@ -559,19 +613,19 @@
             for job in between[h]:
                 job()
         CTXF[base : base + L, :] = GQF[...].astype(BF16)
-        store = local(LIN.at[s], r_["logits_out"].at[s], s)
         parts = [
             wires.send(CTXF.at[theirs(s), :], CTXR.at[0, s], c_dev),
             wires.send(CTXF.at[mine(s), :], CTXR.at[1, s], x_dev),
             wires.send(CTXF.at[theirs(s), :], CTXR.at[2, s], d_dev),
         ]
-        return store, parts
+        return parts
 
     def tile_loop(count, body, init):
         def step(i, carry):
-            return body(pl.multiple_of(i * TILE, TILE), carry)
-
-        return lax.fori_loop(0, count // TILE, step, init)
+            start = pl.multiple_of(i * 2 * TILE, 2 * TILE)
+            return body(start + TILE, body(start, carry))
+
+        return lax.fori_loop(0, count // (2 * TILE), step, init)
 
     def token_rows(s, r):
         return pl.ds(pl.multiple_of(s * L + core * half + r, TILE), TILE)
@@ -747,7 +801,6 @@
             GKF[...] += dot_tn(grad_raw, Q[all_rows, :] * pick)
             for job in between[h]:
                 job()
-        store = local(GLB.at[s], r_["glin_out"].at[s], 2 + s)
         low_q = (GQF[...] * 0.125).astype(BF16)
         low_k = (GKF[...] * 0.125).astype(BF16)
         low_v = GVF[...].astype(BF16)
@@ -761,7 +814,7 @@
         def product(rows):
             return dot_nt(GP[rows, :], WA[:, : 5 * EDGE])
 
-        return store, Reduction(2, s, product)
+        return Reduction(2, s, product)
 
     def token_grads(s, total):
         def body(r, carry):
@@ -774,14 +827,17 @@
 
     class Scatter:
         def __init__(self, tag, fill):
-            self.stage, self.yr = r_["ST" + tag], r_["YR" + tag]
-            self.zs, self.zr = r_["ZS" + tag], r_["ZR" + tag]
+            self.stage, self.yr = getattr(r_, "ST" + tag), getattr(r_, "YR" + tag)
+            self.zs, self.zr = getattr(r_, "ZS" + tag), getattr(r_, "ZR" + tag)
             fill(self.stage)
             self.y_in = [
                 wires.send(self.stage.at[1 - y, zto[k]], self.yr.at[zto[k]], y_dev)
-                for k in (1, 2, 3, 0)
+                for k in range(1, Z)
             ]
             self.sent = []
+
+        def late(self):
+            self.last = wires.send(self.stage.at[1 - y, z], self.yr.at[z], y_dev)
 
         def block(self, index):
             return self.stage[y, index].astype(F32) + self.yr[index].astype(F32)
@@ -796,7 +852,7 @@
                 self.along(k)
 
         def finish(self):
-            self.y_in[Z - 1].wait_recv()
+            self.last.wait_recv()
             total = self.block(z)
             for k in range(1, Z):
                 self.sent[k - 1].wait_recv()
@@ -823,33 +879,48 @@
         fill_blocks(stage, 0, dot_tn(tok[...], GP[:, : 3 * EDGE]).astype(BF16))
 
     def fill_second(stage):
-        keys, outs = dot_tn(tok[...], GP[:, 3 * EDGE :]), r_["OG"]
+        keys, outs = dot_tn(tok[...], GP[:, 3 * EDGE :]), r_.OG
         fill_blocks(stage, 0, keys[:, :EDGE].astype(BF16))
         fill_blocks(stage, EDGE, (keys[:, EDGE:] + outs[:, :EDGE]).astype(BF16))
         fill_blocks(stage, PAIR, outs[:, EDGE:].astype(BF16))
 
     def pass_on(gather, step):
-        return lambda: gather.forward(step)
-
-    store_l0, parts0 = attend(0, ((), (pass_on(gather_u, 0),), (pass_on(gather_d, 0),)))
+        return lambda: gather.step(step)
+
+    parts0 = attend(
+        0,
+        (
+            (pass_on(gather_u, 2), gather_d.across),
+            (gather_e.meet,),
+            (pass_on(gather_d, 1),),
+        ),
+    )
+    parts1 = attend(
+        1,
+        (
+            (pass_on(gather_u, 3),),
+            (pass_on(gather_d, 2), pass_on(gather_e, 1)),
+            (),
+        ),
+    )
     wo_x.wait_recv()
     wo_d = wires.send(WO.at[1], WO.at[2], c_dev)
-    store_l1, parts1 = attend(1, ((pass_on(gather_u, 1),), (pass_on(gather_d, 1),), ()))
-    gather_u.forward(2)
+    gather_e.step(2)
     wo_core.wait_recv()
     wo_d.wait_recv()
     normed0 = out_project(0, parts0)
-    gather_d.forward(2)
-    normed1 = out_project(1, parts1)
+    gather_d.step(3)
     gather_u.finish()
     normed0.wait_recv()
     feed_up(0)
+    gather_e.step(3)
+    normed1 = out_project(1, parts1)
+    gather_d.finish()
+    down0 = feed_down(0)
     normed1.wait_recv()
     feed_up(1)
-    gather_d.finish()
-    down0 = feed_down(0)
+    down0.cross()
     down1 = feed_down(1)
-    down0.cross()
     down0.wait()
     down1.cross()
     branch0, mix0 = norm_two(0, down0)
@@ -868,87 +939,87 @@
     attn0 = norm_one_back(0, back0)
     scatter_d.along(2)
     attn0.wait_recv()
-    store_g0, token0 = attend_back(0, ((), (), ()))
+    token0 = attend_back(0, ((), (), ()))
     token0.cross()
     scatter_d.along(3)
     back1.wait()
     attn1 = norm_one_back(1, back1)
     scatter_u.along(1)
+    norms_core = wires.send(SMG.at[0:8], SMR.at[0], c_dev)
     attn1.wait_recv()
-    r_["OG"][...] = dot_tn(GAT[...], CTXF[...])
+    r_.OG[...] = dot_tn(GAT[...], CTXF[...])
+    norms_core.wait_recv()
+    SMS[0] = SMG[0:8] + SMR[0]
+    norms_y = wires.send(SMS.at[0], SMR.at[1], y_dev)
+    scatter_d.late()
+    scatter_u.late()
 
     def pass_up(step):
         return lambda: scatter_u.along(step)
 
-    store_g1, token1 = attend_back(1, ((), (pass_up(2),), (pass_up(3),)))
-    small_core = wires.send(SMG, SMR.at[0], c_dev)
+    token1 = attend_back(1, ((), (pass_up(2),), (pass_up(3),)))
+    heads_y = wires.send(SMG.at[8:16], SMR.at[5], y_dev)
+    norms_y.wait_recv()
+    SMS[1] = SMS[0] + SMR[1]
+    norms_z = [wires.send(SMS.at[1], SMR.at[1 + k], z_dev[k]) for k in range(1, Z)]
     scatter_f = Scatter("F", fill_first)
-    small_core.wait_recv()
-    upper = lax.broadcasted_iota(jnp.int32, SMG.shape, 0) < 8
-    SMS[0] = SMG[...] + jnp.where(upper, SMR[0], 0.0)
-    small_y = wires.send(SMS.at[0], SMR.at[1], y_dev)
-    scatter_g = Scatter("G", fill_second)
     token0.wait()
     token1.cross()
+    scatter_g = Scatter("G", fill_second)
+    heads_y.wait_recv()
+    SMS[2] = SMG[8:16] + SMR[5]
+    heads_z = [wires.send(SMS.at[2], SMR.at[5 + k], z_dev[k]) for k in range(1, Z)]
     share0 = token_grads(0, token0)
     mix0.wait_recv()
     mix1.wait_recv()
-    store_mix = local(MIX, r_["mixed"], 4)
-    small_y.wait_recv()
-    SMS[1] = SMS[0] + SMR[1]
-    small_z = [wires.send(SMS.at[1], SMR.at[1 + k], z_dev[k]) for k in range(1, Z)]
     scatter_f.along_all()
-    r_["gd"][...] = scatter_d.finish()
-    r_["gu"][...] = scatter_u.finish()
+    scatter_g.along_all()
+    scatter_f.late()
+    scatter_g.late()
+
+    def collect(first, parts, into):
+        value = first
+        for k in range(1, Z):
+            parts[k - 1].wait_recv()
+            value = value + SMR[into + k]
+        return value
+
+    def own(value, count, width, start=0):
+        mine_ = value[:count, start : start + width]
+        for i in range(1, Z * Y):
+            there = value[:count, start + i * width : start + (i + 1) * width]
+            mine_ = jnp.where(dpi == i, there, mine_)
+        return mine_
+
     token1.wait()
     share1 = token_grads(1, token1)
-    scatter_g.along_all()
-    small_total = SMS[1]
-    for k in range(1, Z):
-        small_z[k - 1].wait_recv()
-        small_total = small_total + SMR[1 + k]
-    SMV[...] = small_total
-
-    def own(first, count, width, start=0):
-        value = SMV[first : first + count, start : start + width]
-        for i in range(1, Z * Y):
-            here = SMV[first : first + count, start + i * width : start + (i + 1) * width]
-            value = jnp.where(dpi == i, here, value)
-        return value
-
-    r_["ggains"][...] = own(0, 2, SH)
-    r_["gshifts"][...] = own(2, 4, SH)
-    r_["ghbias"][0:1] = own(8, 1, piece)
-    r_["ghbias"][1:2] = own(9, 1, piece, PAIR - C)
-    r_["gfbias"][...] = own(10, 1, SH)
+    norms = collect(SMS[1], norms_z, 1)
+    r_.ggains[...] = own(norms, 2, SH)
+    r_.gshifts[...] = own(norms[2:6], 4, SH)
+    heads = collect(SMS[2], heads_z, 5)
+    r_.ghbias[0:1] = own(heads[0:1], 1, piece)
+    r_.ghbias[1:2] = own(heads[1:2], 1, piece, PAIR - C)
+    r_.gfbias[...] = own(heads[2:3], 1, SH)
+    r_.gd[...] = scatter_d.finish()
+    r_.gu[...] = scatter_u.finish()
     share0.wait_recv()
     share1.wait_recv()
-    store_gt = local(GT, r_["gtok"], 5)
     first = scatter_f.finish()
-    r_["ga"][0] = first[:, :C]
-    r_["ga"][2] = first[:, C:]
     second = scatter_g.finish()
-    r_["ga"][1] = second[:, :C]
-    r_["go"][...] = jnp.transpose(second[:, C:])
-    for copy in (store_l0, store_l1, store_g0, store_g1, store_mix, store_gt):
-        copy.wait()
+    r_.ga[0] = first[:, :C]
+    r_.ga[2] = first[:, C:]
+    r_.ga[1] = second[:, :C]
+    r_.go[...] = jnp.transpose(second[:, C:])
     wires.drain_all()
 
 
 def pass_kernel(count, *refs):
-    sources, targets = refs[:count], refs[count : 2 * count]
-    held, sem = refs[2 * count : 3 * count], refs[3 * count]
-    loads = [
-        pltpu.make_async_copy(sources[i], held[i], sem.at[i]) for i in range(count)
+    sources, targets, sem = refs[:count], refs[count : 2 * count], refs[2 * count]
+    stores = [
+        pltpu.make_async_copy(sources[i], targets[i], sem.at[i]) for i in range(count)
     ]
-    stores = [
-        pltpu.make_async_copy(held[i], targets[i], sem.at[count + i]) for i in range(count)
-    ]
-    for copy in loads:
+    for copy in stores:
         copy.start()
-    for load, store in zip(loads, stores, strict=True):
-        load.wait()
-        store.start()
     for copy in stores:
         copy.wait()
 
@@ -956,13 +1027,14 @@
 def pass_through(arrays):
     count = len(arrays)
     far = pl.BlockSpec(memory_space=pl.ANY)
+    close = pl.BlockSpec(memory_space=pltpu.VMEM)
     return pl.pallas_call(
         functools.partial(pass_kernel, count),
         out_shape=tuple(jax.ShapeDtypeStruct(a.shape, a.dtype) for a in arrays),
-        in_specs=[far] * count,
+        in_specs=[close] * count,
         out_specs=(far,) * count,
-        scratch_shapes=[pltpu.VMEM(a.shape, a.dtype) for a in arrays]
-        + [pltpu.SemaphoreType.DMA((2 * count,))],
+        scratch_shapes=[pltpu.SemaphoreType.DMA((count,))],
+        compiler_params=pltpu.CompilerParams(vmem_limit_bytes=4 * 1024 * 1024),
     )(*arrays)
 
 
@@ -980,68 +1052,70 @@
     width = max(D, FF)
     dma = pltpu.SemaphoreType.DMA
     vm = pltpu.VMEM
-    inputs = {
-        "tok_far": tokens, "wa": jnp.transpose(w_qkv, (1, 0, 2)), "wo": w_out, "wu": w_up,
-        "wd": w_down.T, "hbias": head_bias, "fbias": ff_bias[None], "gains": norm_gains,
-        "shifts": shift_biases, "seg": segments,
-        "gout": grad_out, "lin": logits_in, "gl": grad_logits,
-    }
-    shape = jax.ShapeDtypeStruct
-    outputs = {
-        "mixed": shape((rows, D), BF16),
-        "logits_out": shape(logits_in.shape, BF16),
-        "gtok": shape((rows, D), BF16),
-        "glin_out": shape(logits_in.shape, BF16),
-        "ga": shape((3, SH, C), F32),
-        "go": shape((C, SH), F32),
-        "gu": shape((SH, FF), F32),
-        "gd": shape((SH, FF), F32),
-        "ghbias": shape(head_bias.shape, F32),
-        "gfbias": shape((1,) + ff_bias.shape, F32),
-        "ggains": shape(norm_gains.shape, F32),
-        "gshifts": shape(shift_biases.shape, F32),
-    }
-    scratch = {
-        "tok": vm((rows, D), BF16),
-        "WA": vm((D, 6 * EDGE), BF16), "PK": vm((SH, 6 * EDGE), BF16), "WU": vm((D, FF), BF16),
-        "WD": vm((D, FF), BF16), "BLEND": vm((16, EDGE), F32),
-        "SMB": vm((16, EDGE), BF16), "SM": vm((16, Z * Y * EDGE), BF16),
-        "SMV": vm((16, width), F32), "HBV": vm((16, 4 * EDGE), F32), "WO": vm((3, D, 2 * EDGE), BF16),
-        "GOUT": vm((seqs, half, D), BF16),
-        "Q": vm((rows, 2 * EDGE), BF16), "K": vm((rows, 2 * EDGE), BF16), "V": vm((rows, 2 * EDGE), BF16),
-        "LIN": vm(logits_in.shape, BF16), "GLB": vm(logits_in.shape, BF16),
-        "PROB": vm((seqs, HEADS, L, 3 * EDGE), BF16), "BIAS": vm((L, 3 * EDGE), F32),
-        "CTXF": vm((rows, 2 * EDGE), BF16), "CTXR": vm((3, seqs, half, 2 * EDGE), BF16),
-        "NORMED": vm((rows, D), BF16), "ACT": vm((rows, FF), BF16), "DG": vm((rows, FF), F32),
-        "BR": vm((rows, D), BF16), "GH": vm((rows, FF), BF16), "GAT": vm((rows, D), BF16),
-        "GC": vm((L, 2 * EDGE), BF16), "MIX": vm((rows, D), BF16), "GT": vm((rows, D), BF16),
-        "XH1": vm((seqs, half, D), F32), "R1": vm((seqs, half, EDGE), F32),
-        "GS": vm((seqs, half, D), F32), "HB": vm((CHUNK, width), F32),
-        "OWN": vm((seqs, half, D), F32), "CS": vm((seqs, half, D), BF16),
-        "CR": vm((seqs, half, D), BF16), "XS": vm((seqs, half, D), BF16),
-        "XR": vm((3, seqs, half, D), BF16), "GP": vm((rows, 5 * EDGE), BF16), "OG": vm((D, 2 * EDGE), F32),
-        "GQF": vm((L, 2 * EDGE), F32), "GKF": vm((L, 2 * EDGE), F32), "GVF": vm((L, 2 * EDGE), F32),
-        "SMG": vm((16, width), F32), "SMS": vm((2, 16, width), F32), "SMR": vm((5, 16, width), F32),
-        "send_sem": dma((COPIES,)), "recv_sem": dma((COPIES,)), "local_sem": dma((8,)),
-    }
+    inputs = dict(
+        tok_far=tokens, wa_far=jnp.transpose(w_qkv, (1, 0, 2)), wo_far=w_out,
+        wu=w_up, wd=w_down.T, hbias_far=head_bias, fbias_far=ff_bias[None],
+        gains_far=norm_gains, shifts_far=shift_biases, seg_far=segments,
+        gout=grad_out, lin=logits_in, gl=grad_logits,
+    )
+    outputs = dict(
+        mixed=vm((rows, D), BF16),
+        logits_out=vm(logits_in.shape, BF16),
+        gtok=vm((rows, D), BF16),
+        glin_out=vm(logits_in.shape, BF16),
+        ga=vm((3, SH, C), F32),
+        go=vm((C, SH), F32),
+        gu=vm((SH, FF), F32),
+        gd=vm((SH, FF), F32),
+        ghbias=vm(head_bias.shape, F32),
+        gfbias=vm((1,) + ff_bias.shape, F32),
+        ggains=vm(norm_gains.shape, F32),
+        gshifts=vm(shift_biases.shape, F32),
+    )
+    scratch = dict(
+        tok=vm((rows, D), BF16), wa=vm((3, SH, C), BF16), wo=vm((C, SH), BF16),
+        hbias=vm(head_bias.shape, BF16), fbias=vm((1,) + ff_bias.shape, BF16),
+        gains=vm(norm_gains.shape, BF16), shifts=vm(shift_biases.shape, BF16),
+        seg=vm(segments.shape, jnp.int32),
+        WA=vm((D, 6 * EDGE), BF16), WU=vm((D, FF), BF16),
+        WD=vm((D, FF), BF16), BLEND=vm((16, EDGE), F32),
+        SM=vm((16, Z * Y * EDGE), BF16),
+        SMV=vm((16, width), F32), HBV=vm((16, 4 * EDGE), F32), WO=vm((3, D, 2 * EDGE), BF16),
+        GOUT=vm((seqs, half, D), BF16),
+        Q=vm((rows, 2 * EDGE), BF16), K=vm((rows, 2 * EDGE), BF16), V=vm((rows, 2 * EDGE), BF16),
+
+        PROB=vm((seqs, HEADS, L, 3 * EDGE), BF16), BIAS=vm((L, 3 * EDGE), F32),
+        CTXF=vm((rows, 2 * EDGE), BF16), CTXR=vm((3, seqs, half, 2 * EDGE), BF16),
+        NORMED=vm((rows, D), BF16), ACT=vm((rows, FF), BF16), DG=vm((rows, FF), F32),
+        BR=vm((rows, D), BF16), GH=vm((rows, FF), BF16), GAT=vm((rows, D), BF16),
+        GC=vm((L, 2 * EDGE), BF16),
+        XH1=vm((seqs, half, D), F32), R1=vm((seqs, half, EDGE), F32),
+        GS=vm((seqs, half, D), F32), HB=vm((CHUNK, width), F32),
+        OWN=vm((seqs, half, D), F32), CS=vm((seqs, half, D), BF16),
+        CR=vm((seqs, half, D), BF16), XS=vm((seqs, half, D), BF16),
+        XR=vm((3, seqs, half, D), BF16), GP=vm((rows, 5 * EDGE), BF16), OG=vm((D, 2 * EDGE), F32),
+        GQF=vm((L, 2 * EDGE), F32), GKF=vm((L, 2 * EDGE), F32), GVF=vm((L, 2 * EDGE), F32),
+        SMG=vm((16, width), F32), SMS=vm((3, 8, width), F32), SMR=vm((9, 8, width), F32),
+        send_sem=dma((SENDS,)), recv_sem=dma((ARRIVALS,)), local_sem=dma((LOADS,)),
+    )
     for tag in "UDFG":
         block = (SH, FF if tag in "UD" else 3 * EDGE)
         scratch["ST" + tag] = vm((Y, Z) + block, BF16)
         scratch["YR" + tag] = vm((Z,) + block, BF16)
         scratch["ZS" + tag] = vm((Z - 1,) + block, BF16)
         scratch["ZR" + tag] = vm((Z - 1,) + block, BF16)
-    near, far = pl.BlockSpec(memory_space=pltpu.VMEM), pl.BlockSpec(memory_space=pl.ANY)
-    distant = ("tok_far", "gout", "lin", "gl", "mixed", "logits_out", "gtok", "glin_out")
+    far = pl.BlockSpec(memory_space=pl.ANY)
+    close = pl.BlockSpec(memory_space=pltpu.VMEM)
     names = (*inputs, *outputs, *scratch)
     dims = (L, HEADS, HD, D, FF, C, SH)
     results = pl.pallas_call(
         functools.partial(layer_kernel, names, dims),
         out_shape=tuple(outputs.values()),
-        in_specs=[far if name in distant else near for name in inputs],
-        out_specs=tuple(far if name in distant else near for name in outputs),
+        in_specs=[far] * len(inputs),
+        out_specs=(close,) * len(outputs),
         scratch_shapes=list(scratch.values()),
         compiler_params=pltpu.CompilerParams(
-            collective_id=0, has_side_effects=True, vmem_limit_bytes=66 * 1000 * 1000
+            collective_id=0, has_side_effects=True, vmem_limit_bytes=52 * 1024 * 1024
         ),
     )(*inputs.values())
     mixed, logits_out, gtok, glin, ga, go, gu, gd, ghbias, gfbias, ggains, gshifts = pass_through(

time: 155 us -> 132 us (0.85)
  Pallas kernels: 154 us -> 131 us
    pallas_call x1, Pallas kernels: 145 us -> 127 us  [fused_shards(): pl.pallas_call(functools.partial(layer_kernel, names, dims), out_shape=tu...]
    pallas_call x1, Pallas kernels: 8.21 us -> 4.02 us  [pass_through(): pl.pallas_call(functools.partial(pass_kernel, count), out_shape=tuple((ja...]
where the time goes in v3:
time: 132 us
  Pallas kernels  131 us (99%)
    pallas_call x1, Pallas kernels, fused_shards(): pl.pallas_call(functools.partial(layer_kernel, names, dims), out_shape=tu...  127 us
    pallas_call x1, Pallas kernels, pass_through(): pl.pallas_call(functools.partial(pass_kernel, count), out_shape=tuple((ja...  4.02 us

profile of v3, /device:TPU:0, one launch (start us, length us, event | category | flops | bytes accessed | tf_op | source)
XLA Modules:
  0.0 132.2 jit_solution(6384969863261461965)
XLA Ops:
  0.6 127.4 %shard_map.220 = (bf16[1024,768]{1,0:T(8,128)(2,1)S(1)}, bf16[2,3,512,512]{3,2,1,0:T(8,128)(2,1)S(1)}, bf16[1024,768]{1,0:T(8,128)(2,1)S(1)}, bf16[2,3,512,512]{...) custom-call(bf16[1024,768]{1,0:T(8,128)(2,1)} %refs_0_.1, ...), custom_call_target="tpu_custom_call" | custom-call | tf_op jit(solution)/shard_map/pallas_call | solution.py:1111
  128.0 4.0 %shard_map.221 = (bf16[1024,768]{1,0:T(8,128)(2,1)}, bf16[2,3,512,512]{3,2,1,0:T(8,128)(2,1)}, bf16[1024,768]{1,0:T(8,128)(2,1)}, bf16[2,3,512,512]{3,2,1,0:T(8,...) custom-call(bf16[1024,768]{1,0:T(8,128)(2,1)S(1)} %get-tuple-element, ...), custom_call_target="tpu_custom_call" | custom-call | tf_op jit(solution)/shard_map/pallas_call | solution.py:1031

commit v4 on v3

--- a/solution.py
+++ b/solution.py
@@ -296,8 +296,9 @@
         self.describe(ref, ref, device, 0, into).wait_recv()
 
     def drain(self, copy):
-        copy.wait_send()
-        self.drained.append(copy)
+        if not any(copy is done for done in self.drained):
+            copy.wait_send()
+            self.drained.append(copy)
 
     def drain_all(self):
         for copy in self.sent:
@@ -890,39 +891,34 @@
     parts0 = attend(
         0,
         (
-            (pass_on(gather_u, 2), gather_d.across),
-            (gather_e.meet,),
+            (gather_d.across,),
+            (pass_on(gather_u, 2), gather_e.meet),
             (pass_on(gather_d, 1),),
         ),
     )
-    parts1 = attend(
-        1,
-        (
-            (pass_on(gather_u, 3),),
-            (pass_on(gather_d, 2), pass_on(gather_e, 1)),
-            (),
-        ),
-    )
+    parts1 = attend(1, ((pass_on(gather_u, 3),), (), (pass_on(gather_d, 2),)))
     wo_x.wait_recv()
     wo_d = wires.send(WO.at[1], WO.at[2], c_dev)
-    gather_e.step(2)
     wo_core.wait_recv()
     wo_d.wait_recv()
     normed0 = out_project(0, parts0)
-    gather_d.step(3)
+    gather_e.step(1)
     gather_u.finish()
     normed0.wait_recv()
+    gather_d.step(3)
     feed_up(0)
+    gather_e.step(2)
+    normed1 = out_project(1, parts1)
     gather_e.step(3)
-    normed1 = out_project(1, parts1)
     gather_d.finish()
     down0 = feed_down(0)
     normed1.wait_recv()
     feed_up(1)
     down0.cross()
     down1 = feed_down(1)
+    wires.drain(down0.far)
+    down1.cross()
     down0.wait()
-    down1.cross()
     branch0, mix0 = norm_two(0, down0)
     branch0.wait_recv()
     back0 = feed_back(0)
@@ -933,17 +929,17 @@
     scatter_d = Scatter("D", fill_square(BR, ACT))
     back1 = feed_back(1)
     scatter_u = Scatter("U", fill_square(NORMED, GH))
+    back1.cross()
     scatter_d.along(1)
     back0.wait()
-    back1.cross()
     attn0 = norm_one_back(0, back0)
     scatter_d.along(2)
     attn0.wait_recv()
     token0 = attend_back(0, ((), (), ()))
-    token0.cross()
     scatter_d.along(3)
     back1.wait()
     attn1 = norm_one_back(1, back1)
+    token0.cross()
     scatter_u.along(1)
     norms_core = wires.send(SMG.at[0:8], SMR.at[0], c_dev)
     attn1.wait_recv()
@@ -952,28 +948,28 @@
     SMS[0] = SMG[0:8] + SMR[0]
     norms_y = wires.send(SMS.at[0], SMR.at[1], y_dev)
     scatter_d.late()
-    scatter_u.late()
 
     def pass_up(step):
         return lambda: scatter_u.along(step)
 
     token1 = attend_back(1, ((), (pass_up(2),), (pass_up(3),)))
     heads_y = wires.send(SMG.at[8:16], SMR.at[5], y_dev)
+    scatter_f = Scatter("F", fill_first)
     norms_y.wait_recv()
     SMS[1] = SMS[0] + SMR[1]
     norms_z = [wires.send(SMS.at[1], SMR.at[1 + k], z_dev[k]) for k in range(1, Z)]
-    scatter_f = Scatter("F", fill_first)
-    token0.wait()
     token1.cross()
     scatter_g = Scatter("G", fill_second)
     heads_y.wait_recv()
     SMS[2] = SMG[8:16] + SMR[5]
     heads_z = [wires.send(SMS.at[2], SMR.at[5 + k], z_dev[k]) for k in range(1, Z)]
+    token0.wait()
     share0 = token_grads(0, token0)
     mix0.wait_recv()
     mix1.wait_recv()
     scatter_f.along_all()
     scatter_g.along_all()
+    scatter_u.late()
     scatter_f.late()
     scatter_g.late()
 

time: 132 us -> 128 us (0.970)
  Pallas kernels: 131 us -> 127 us
    pallas_call x1, Pallas kernels: 127 us -> 123 us  [fused_shards(): pl.pallas_call(functools.partial(layer_kernel, names, dims), out_shape=tu...]
where the time goes in v4:
time: 128 us
  Pallas kernels  127 us (99%)
    pallas_call x1, Pallas kernels, fused_shards(): pl.pallas_call(functools.partial(layer_kernel, names, dims), out_shape=tu...  123 us
    pallas_call x1, Pallas kernels, pass_through(): pl.pallas_call(functools.partial(pass_kernel, count), out_shape=tuple((ja...  4.02 us

profile of v4, /device:TPU:0, one launch (start us, length us, event | category | flops | bytes accessed | tf_op | source)
XLA Modules:
  0.0 128.0 jit_solution(15449931056939012956)
XLA Ops:
  0.6 123.2 %shard_map.220 = (bf16[1024,768]{1,0:T(8,128)(2,1)S(1)}, bf16[2,3,512,512]{3,2,1,0:T(8,128)(2,1)S(1)}, bf16[1024,768]{1,0:T(8,128)(2,1)S(1)}, bf16[2,3,512,512]{...) custom-call(bf16[1024,768]{1,0:T(8,128)(2,1)} %refs_0_.1, ...), custom_call_target="tpu_custom_call" | custom-call | tf_op jit(solution)/shard_map/pallas_call | solution.py:1107
  123.9 4.0 %shard_map.221 = (bf16[1024,768]{1,0:T(8,128)(2,1)}, bf16[2,3,512,512]{3,2,1,0:T(8,128)(2,1)}, bf16[1024,768]{1,0:T(8,128)(2,1)}, bf16[2,3,512,512]{3,2,1,0:T(8,...) custom-call(bf16[1024,768]{1,0:T(8,128)(2,1)S(1)} %get-tuple-element, ...), custom_call_target="tpu_custom_call" | custom-call | tf_op jit(solution)/shard_map/pallas_call | solution.py:1027
